TPU v7x, 128 devices: a whole 4x4x4 slice. The times are simulated.
128 devices in a mesh: layer: 4 (over z_hi, core), dp: 32 (over y, z_lo, x).
Axes of the slice: x: 4, y: 4, z: 4 (z_hi: 2, z_lo: 2; z = z_hi * 2 + z_lo), core: 2. Of those that a mesh axis runs over, the one named last changes fastest.
Arguments:
- out_grads: bfloat16 [4, 128, 16384], P('layer', None, 'dp'), may hold values from -3 to 3
- in_acts: bfloat16 [4, 128, 4096], P('layer', None, 'dp'), may hold values from -3 to 3
- out_basis: bfloat16 [4, 16384, 16384], P('layer', None, 'dp'), may hold values from -0.046875 to 0.046875
- in_basis: bfloat16 [4, 4096, 4096], P('layer', None, 'dp'), may hold values from -0.09375 to 0.09375
- eigenvalues: bfloat16 [4, 16384, 4096], P('layer', 'dp'), may hold values from 0.5 to 50
- out_store: bfloat16 [4, 64, 32, 16384], P('layer', 'dp'), may hold values from -0.046875 to 0.046875
- in_store: bfloat16 [4, 64, 32, 4096], P('layer', 'dp'), may hold values from -0.09375 to 0.09375
- counts: int32 [64], P('dp'), may hold values from 1 to 4096
- winners: int32 [4, 6], replicated, may hold values from 0 to 63
Outputs:
- influence: float32 [4, 6, 32], replicated
All inputs are finite; a program needn't handle non-finite values.
Results may differ from a plain program's by a relative error of at most 0.0055.
Values may be sent and summed in bfloat16 or wider, within the bound.
No kernel may reach another device: no remote copies, remote signals or barrier semaphores. Data moves between devices by JAX's collectives and lax.ppermute only.
A program may use at most 192 MiB of HBM per device.

v0:
```python
import functools

import jax
import jax.numpy as jnp
from jax import lax
from jax.sharding import Mesh
from jax.sharding import PartitionSpec as P

NQ = 4
TQ = 32
WIN = 6
R = 32
SPAN = 128
DP = ("dp_0", "dp_1", "dp_2")
LAYER_DP = ("layer_0", "layer_1", "dp_0", "dp_1", "dp_2")
LAYER = ("layer_0", "layer_1")


damping = 0.1


def in_order(blocks, dim):
    blocks = jnp.moveaxis(blocks, 0, dim)
    shape = blocks.shape
    return blocks.reshape(*shape[:dim], shape[dim] * shape[dim + 1], *shape[dim + 2 :])


def all_blocks(value, axes, turns):
    blocks = value[None]
    for k in turns:
        blocks = lax.all_gather(blocks, axes[k], axis=0, tiled=True)
    block = [lax.axis_size(axes[k]) for k in reversed(turns)]
    blocks = blocks.reshape(*block, *value.shape)
    turned = sorted(range(len(turns)), key=lambda place: turns[len(turns) - 1 - place])
    return blocks.transpose(*turned, *range(len(turns), blocks.ndim)).reshape(-1, *value.shape)


def whole_of(value, axes, turns, dim):
    return in_order(all_blocks(value, axes, turns), dim)


def from_everyone(value, axis):
    count = lax.axis_size(axis)
    return lax.all_to_all(
        jnp.broadcast_to(value[None], (count, *value.shape)), axis, 0, 0, tiled=True
    )


def collect(value, axis, dim):
    return in_order(from_everyone(value, axis), dim)


def over_axes(value, axes):
    return functools.reduce(lax.psum, axes, value)


def on_device(
    out_grads, in_acts, out_basis, in_basis, eigenvalues, out_store, in_store, counts, winners
):
    out_local = out_basis[0]
    in_local = in_basis[0]
    out_width = out_local.shape[1]
    rows = out_local
    turned_out = jnp.dot(
        whole_of(out_grads[0], DP, (1, 0, 2), 1), rows, preferred_element_type=jnp.float32
    ).astype(jnp.bfloat16)
    rows = in_local
    turned_part = jnp.dot(
        collect(in_acts[0], DP, 1), rows, preferred_element_type=jnp.float32
    ).astype(jnp.bfloat16)
    turned_in = collect(turned_part, DP, 1)
    left = turned_out.reshape(NQ, TQ, out_width)
    right = turned_in.reshape(NQ, TQ, turned_in.shape[1])
    product = jnp.einsum("qtf,qtd->qfd", left, right, preferred_element_type=jnp.float32)
    divisor = eigenvalues[0].astype(jnp.float32) + damping
    precond = (product / divisor[None]).astype(jnp.bfloat16)
    alive = (jnp.arange(R, dtype=jnp.int32)[None, :] * SPAN < counts[:, None]).astype(jnp.bfloat16)
    masked = in_store[0] * alive[:, :, None]
    out_slices = lax.all_to_all(out_store[0], DP, split_axis=2, concat_axis=0, tiled=True)
    chosen = winners.reshape(NQ * WIN)
    left_rows = jnp.take(out_slices, chosen, axis=0).reshape(NQ, WIN * R, out_width)
    full_width = turned_in.shape[1]
    in_whole = lax.all_gather(masked, DP, axis=0, tiled=True)
    right_rows = jnp.take(in_whole, chosen, axis=0).reshape(NQ, WIN * R, full_width)
    mapped = jnp.einsum("qfd,qkd->qkf", precond, right_rows, preferred_element_type=jnp.float32)
    partial_value = jnp.sum(mapped * left_rows.astype(jnp.float32), axis=2)
    totals = over_axes(partial_value, LAYER_DP)
    return totals.reshape(NQ, WIN, R)


def solution(mesh):
    torus = Mesh(
        mesh.devices.reshape(2, 2, 4, 2, 4), ("layer_0", "layer_1", "dp_0", "dp_1", "dp_2")
    )
    return jax.shard_map(
        on_device,
        mesh=torus,
        in_specs=(
            P(LAYER, None, DP),
            P(LAYER, None, DP),
            P(LAYER, None, DP),
            P(LAYER, None, DP),
            P(LAYER, DP, None),
            P(LAYER, DP, None, None),
            P(LAYER, DP, None, None),
            P(DP),
            P(),
        ),
        out_specs=P(),
        check_vma=False,
    )
```

profile of v0, /device:TPU:8, one launch (start us, length us, event | category | flops | bytes accessed | tf_op | source)
XLA Modules:
  0.0 420.0 jit_solution(17354535812470855363)
XLA Ops:
  6.5 0.0 copy-start
  6.5 0.0 all-gather.6.cloned.1.call-start
  6.5 8.0 %all_gather.13 = bf16[2,128,512]{2,1,0:T(8,128)(2,1)} all-gather(bf16[1,128,512]{2,1,0:T(8,128)(2,1)} %param.9), channel_id=1, replica_groups=mesh['layer_0'=2,'layer_1'=2,'dp_0'=4,'dp_1'=2,'dp_2'=4] {'dp_1'}, dimensions={0}, use_global_device_ids=true | all-gather | bytes 393216 | tf_op jit(solution)/shard_map/all_gather | solution.py:31
  14.5 0.0 all-gather.6.cloned.1.call-update
  14.6 0.0 all-gather.8.cloned.1.call-start
  14.6 24.9 %all-gather.6.cloned.1.call-done = bf16[8,128,512]{2,1,0:T(8,128)(2,1)} async-done(((bf16[2,128,512]{2,1,0:T(8,128)(2,1)}), bf16[8,128,512]{2,1,0:T(8,128)(2,1)}) %all-gather.6.cloned.1.call-update) | async-done | bytes 1048592 | tf_op jit(solution)/shard_map/all_gather | solution.py:31
  39.5 0.0 all-gather.8.cloned.1.call-update
  39.5 0.0 all-gather.4.cloned.1.call-start
  39.6 0.7 compare_convert_fusion
  40.3 2.0 bitcast_multiply_fusion
  42.3 0.0 all-gather.4.cloned.1.call-update
  42.3 0.9 copy.20
  43.2 1.2 broadcast_in_dim.46
  44.4 8.6 %all-to-all-start = ((bf16[32,128,128]{1,2,0:T(8,128)(2,1)}), bf16[32,128,128]{1,2,0:T(8,128)(2,1)S(1)}, u32[]{:S(2)}, u32[]{:S(2)}) async-start(bf16[32,128,128]{1,2,0:T(8,128)(2,1)} %broadcast_in_dim.46), calls=%async_computation | async-start | bytes 2097152 | tf_op jit(solution)/shard_map/all_to_all | solution.py:44
  53.0 17.2 %copy.22 = bf16[1,2,32,16384]{2,1,3,0:T(2,128)(2,1)} copy(bf16[1,2,32,16384]{3,2,1,0:T(8,128)(2,1)} %param.14) | data formatting | bytes 4194304 | tf_op args[5]
  70.2 8.0 %bitcast_bitcast_fusion = bf16[16384,2,32]{2,1,0:T(2,128)(2,1)} fusion(bf16[1,2,32,16384]{2,1,3,0:T(2,128)(2,1)} %copy.22), kind=kLoop, calls=%fused_computation.22 | loop fusion | bytes 4194304
  78.2 0.0 copy-start.3
  78.2 18.2 %reshape.123 = bf16[32,2,16384]{2,1,0:T(2,128)(2,1)} reshape(bf16[16384,2,32]{2,1,0:T(2,128)(2,1)} %bitcast_bitcast_fusion) | data formatting | bytes 4194304
  96.4 0.0 all-to-all-done
  96.4 0.0 copy-start.2
  96.4 1.0 copy-done.2
  97.3 8.3 %all-to-all-start.2 = ((bf16[32,2,16384]{2,1,0:T(2,128)(2,1)}), bf16[32,2,16384]{2,1,0:T(2,128)(2,1)S(1)}, u32[]{:S(2)}, u32[]{:S(2)}) async-start(bf16[32,2,16384]{2,1,0:T(2,128)(2,1)} %reshape.123), calls=%async_computation.2 | async-start | bytes 4194304 | tf_op jit(solution)/shard_map/all_to_all | solution.py:79
  105.6 0.0 copy-done.3
  105.7 0.1 reshape.100
  105.7 0.1 broadcast_in_dim.41
  105.8 0.1 broadcast_in_dim.42
  105.9 0.0 copy-done
  105.9 1.7 convolution_convert_fusion
  107.6 41.9 %all-to-all-done.2 = bf16[32,2,16384]{2,1,0:T(2,128)(2,1)S(1)} async-done(((bf16[32,2,16384]{2,1,0:T(2,128)(2,1)}), bf16[32,2,16384]{2,1,0:T(2,128)(2,1)S(1)}, u32[]{:S(2)}, u32[]{:S(2)}) %all-to-all-start.2) | async-done | bytes 2097184 | tf_op jit(solution)/shard_map/all_to_all | solution.py:79
  149.6 1.2 broadcast_in_dim.47
  150.8 7.3 %all-to-all-start.1 = ((bf16[32,128,128]{2,1,0:T(8,128)(2,1)}), bf16[32,128,128]{2,1,0:T(8,128)(2,1)S(1)}, u32[]{:S(2)}, u32[]{:S(2)}) async-start(bf16[32,128,128]{2,1,0:T(8,128)(2,1)} %broadcast_in_dim.47), calls=%async_computation.1 | async-start | bytes 2097152 | tf_op jit(solution)/shard_map/all_to_all | solution.py:44
  158.1 6.6 %add_bitcast_fusion = f32[512,4096]{1,0:T(8,128)} fusion(bf16[1,512,4096]{2,1,0:T(8,128)(2,1)} %param.13), kind=kLoop, calls=%fused_computation.6 | loop fusion | flops 4194304 | bytes 12582912 | tf_op jit(solution)/shard_map/div | solution.py:76
  164.6 6.6 %reshape.124 = bf16[16384,2,32]{2,1,0:T(2,128)(2,1)} reshape(bf16[32,2,16384]{2,1,0:T(2,128)(2,1)S(1)} %all-to-all-done.2) | data formatting | bytes 4194304
  171.2 17.8 %copy.27 = bf16[2,32,32,512]{3,1,0,2:T(8,128)(2,1)} copy(bf16[2,32,32,512]{1,0,3,2:T(2,128)(2,1)} %bitcast.56) | data formatting | bytes 4194304 | tf_op jit(solution)/shard_map/all_to_all | solution.py:79
  189.0 129.3 %all-to-all-done.1 = bf16[32,128,128]{2,1,0:T(8,128)(2,1)S(1)} async-done(((bf16[32,128,128]{2,1,0:T(8,128)(2,1)}), bf16[32,128,128]{2,1,0:T(8,128)(2,1)S(1)}, u32[]{:S(2)}, u32[]{:S(2)}) %all-to-all-start.1) | async-done | bytes 1048608 | tf_op jit(solution)/shard_map/all_to_all | solution.py:44
  318.4 0.7 copy.21
  319.0 0.5 reshape_reshape.3
  319.5 2.2 gather_fusion.1
  321.7 0.2 bitcast_select_fusion.1
  321.9 0.0 all-gather.8.cloned.1.call-done
  321.9 4.6 %copy.18 = bf16[4,2,4,128,512]{4,3,2,1,0:T(8,128)(2,1)} copy(bf16[4,2,4,128,512]{4,3,1,0,2:T(8,128)(2,1)} %bitcast.60) | data formatting | bytes 8388608 | tf_op jit(solution)/shard_map/transpose | solution.py:35
  326.5 6.4 %copy.19 = bf16[128,32,512]{0,2,1:T(8,128)(2,1)} copy(bf16[128,32,512]{2,0,1:T(8,128)(2,1)} %bitcast.59) | data formatting | bytes 8388608 | tf_op jit(solution)/shard_map/transpose | solution.py:23
  332.9 9.4 %fusion.5 = bf16[128,512]{1,0:T(8,128)(2,1)S(1)} fusion(bf16[128,16384]{0,1:T(8,128)(2,1)} %bitcast.58, bf16[1,16384,512]{2,1,0:T(8,128)(2,1)} %param.11), kind=kOutput, calls=%fused_computation.10 | convolution fusion | flops 2147549184 | bytes 21102592 | tf_op jit(solution)/shard_map/dot_general | solution.py:64
  342.4 0.0 all-gather.4.cloned.1.call-done
  342.4 10.2 %gather_fusion = bf16[24,32,4096]{2,1,0:T(8,128)(2,1)} fusion(bf16[64,32,4096]{2,1,0:T(8,128)(2,1)} %all-gather.4.cloned.1.call-done, s32[1024]{0:T(1024)S(1)} %pad_clamp_fusion), kind=kCustom, calls=%fused_computation | custom fusion | bytes 12583008 | tf_op jit(solution)/shard_map/jit(_take)/gather | solution.py:84
  352.6 6.1 %bitcast_select_fusion = bf16[4,192,4096]{2,1,0:T(8,128)(2,1)} fusion(pred[4,192]{1,0:T(4,128)(4,1)S(1)} %broadcast_in_dim.42, bf16[4,192,4096]{2,1,0:T(8,128)(2,1)} %bitcast.57), kind=kLoop, calls=%fused_computation.7 | loop fusion | flops 3145728 | bytes 12583680 | tf_op jit(solution)/shard_map/jit(_take)/select_n | solution.py:84
  358.7 0.0 copy-start.1
  358.7 14.6 %fusion.4 = f32[4,192]{1,0:T(4,128)S(1)} fusion(bf16[4,192,512]{2,1,0:T(8,128)(2,1)S(1)} %bitcast_select_fusion.1, bf16[4,192,4096]{2,1,0:T(8,128)(2,1)} %bitcast_select_fusion, f32[512,4096]{1,0:T(8,128)} %add_bitcast_fusion, bf16[4,32,512]{2,1,0:T(8,128)(2,1)S(1)} %bitcast.65, bf16[4,32,4096]{2,1,0:T(8,128)(2,1)S(1)} %reshape_reshape.3), kind=kOutput, calls=%fused_computation.9 | convolution fusion | flops 3776052480 | bytes 16649216 | tf_op jit(solution)/shard_map/qfd,qkd->qkf/dot_general | solution.py:85
  373.2 6.4 %psum.35 = f32[4,192]{1,0:T(4,128)S(1)} all-reduce(f32[4,192]{1,0:T(4,128)S(1)} %fusion.4), channel_id=1, replica_groups=mesh['layer_0'=2,'layer_1'=2,'dp_0'=4,'dp_1'=2,'dp_2'=4] {'layer_0'}, use_global_device_ids=true, to_apply=%region_1.2 | all-reduce | flops 768 | bytes 6144 | tf_op jit(solution)/shard_map/psum | solution.py:54
  379.7 2.4 psum.36
  382.1 11.5 %psum.37 = f32[4,192]{1,0:T(4,128)S(1)} all-reduce(f32[4,192]{1,0:T(4,128)S(1)} %psum.36), channel_id=1, replica_groups=mesh['layer_0'=2,'layer_1'=2,'dp_0'=4,'dp_1'=2,'dp_2'=4] {'dp_0'}, use_global_device_ids=true, to_apply=%region_3.4 | all-reduce | flops 768 | bytes 6144 | tf_op jit(solution)/shard_map/psum | solution.py:54
  393.6 4.9 %psum.38 = f32[4,192]{1,0:T(4,128)S(1)} all-reduce(f32[4,192]{1,0:T(4,128)S(1)} %psum.37), channel_id=1, replica_groups=mesh['layer_0'=2,'layer_1'=2,'dp_0'=4,'dp_1'=2,'dp_2'=4] {'dp_1'}, use_global_device_ids=true, to_apply=%region_4.5 | all-reduce | flops 768 | bytes 6144 | tf_op jit(solution)/shard_map/psum | solution.py:54
  398.5 0.1 reshape.106
  398.6 14.3 %psum.39 = f32[4,6,32]{2,1,0:T(8,128)S(1)} all-reduce(f32[4,6,32]{2,1,0:T(8,128)S(1)} %reshape.106), channel_id=1, replica_groups=mesh['layer_0'=2,'layer_1'=2,'dp_0'=4,'dp_1'=2,'dp_2'=4] {'dp_2'}, use_global_device_ids=true, to_apply=%region_5.6 | all-reduce | flops 768 | bytes 6144 | tf_op jit(solution)/shard_map/psum | solution.py:54
  412.9 0.6 copy.25
  413.5 0.0 copy-done.1
  (4 shorter events, 0.0 us)
Async XLA Ops:
  6.5 99.4 %copy-start = (bf16[1,4096,128]{2,1,0:T(8,128)(2,1)S(1)}, bf16[1,4096,128]{2,1,0:T(8,128)(2,1)}, u32[]{:S(2)}) copy-start(bf16[1,4096,128]{2,1,0:T(8,128)(2,1)} %param.12) | copy-start | bytes 3145732
  6.5 33.0 %all-gather.6.cloned.1.call-start = ((), (), s32[]{:S(2)}) async-start(), calls=%async_computation.4 | async-start | bytes 1310720 | tf_op jit(solution)/shard_map/all_gather | solution.py:31
  14.6 307.4 %all-gather.8.cloned.1.call-start = ((), (), s32[]{:S(2)}) async-start(), calls=%async_computation.5 | async-start | bytes 5242880 | tf_op jit(solution)/shard_map/all_gather | solution.py:31
  39.5 302.9 %all-gather.4.cloned.1.call-start = ((), (), s32[]{:S(2)}) async-start(), calls=%async_computation.3 | async-start | bytes 17301504 | tf_op jit(solution)/shard_map/all_gather | solution.py:83
  44.4 52.0 %all-to-all-start = ((bf16[32,128,128]{1,2,0:T(8,128)(2,1)}), bf16[32,128,128]{1,2,0:T(8,128)(2,1)S(1)}, u32[]{:S(2)}, u32[]{:S(2)}) async-start(bf16[32,128,128]{1,2,0:T(8,128)(2,1)} %broadcast_in_dim.46), calls=%async_computation | async-start | bytes 2097152 | tf_op jit(solution)/shard_map/all_to_all | solution.py:44
  78.2 27.4 %copy-start.3 = (s32[4,6]{1,0:T(4,128)S(1)}, s32[4,6]{1,0:T(4,128)}, u32[]{:S(2)}) copy-start(s32[4,6]{1,0:T(4,128)} %param.17) | copy-start | bytes 292
  96.4 1.0 copy-start.2
  97.3 52.2 %all-to-all-start.2 = ((bf16[32,2,16384]{2,1,0:T(2,128)(2,1)}), bf16[32,2,16384]{2,1,0:T(2,128)(2,1)S(1)}, u32[]{:S(2)}, u32[]{:S(2)}) async-start(bf16[32,2,16384]{2,1,0:T(2,128)(2,1)} %reshape.123), calls=%async_computation.2 | async-start | bytes 4194304 | tf_op jit(solution)/shard_map/all_to_all | solution.py:79
  150.8 167.6 %all-to-all-start.1 = ((bf16[32,128,128]{2,1,0:T(8,128)(2,1)}), bf16[32,128,128]{2,1,0:T(8,128)(2,1)S(1)}, u32[]{:S(2)}, u32[]{:S(2)}) async-start(bf16[32,128,128]{2,1,0:T(8,128)(2,1)} %broadcast_in_dim.47), calls=%async_computation.1 | async-start | bytes 2097152 | tf_op jit(solution)/shard_map/all_to_all | solution.py:44
  358.7 54.8 %copy-start.1 = (bf16[1,4096,128]{2,1,0:T(8,128)(2,1)S(1)}, bf16[1,4096,128]{2,1,0:T(8,128)(2,1)}, u32[]{:S(2)}) copy-start(bf16[1,4096,128]{2,1,0:T(8,128)(2,1)} %param.12) | copy-start | bytes 3145732
Sparse Core Ops, SparseCore 0:
  14.7 24.7 all-gather.5
  41.2 58.4 all-gather.7
  101.3 218.5 all-gather.3
where the time goes:
time: 422 us; the launch traced here: 420 us
  waiting for transfers between devices  196 us (46%)
  local copies, waits for them, and re-layouts  97.6 us (23%)
  blocking collectives  47.6 us (11%)
  matrix products  25.7 us (6%)
  starting transfers between devices  24.3 us (6%)
  other arithmetic  15.5 us (4%)
  between operations  13.2 us (3%)
    all_to_all x2, waiting for transfers between devices, from_everyone(): lax.all_to_all(jnp.broadcast_to(value[None], (count, *value.shape)), axis...  129 us
    unnamed x12, local copies, waits for them, and re-layouts  50.9 us
    all_to_all x1, waiting for transfers between devices, on_device(): lax.all_to_all(out_store[0], DP, split_axis=2, concat_axis=0, tiled=True)  41.9 us
    psum x5, blocking collectives, over_axes(): return functools.reduce(lax.psum, axes, value)  39.6 us
    all_gather x2, waiting for transfers between devices, all_blocks(): blocks = lax.all_gather(blocks, axes[k], axis=0, tiled=True)  24.9 us
    all_to_all x1, local copies, waits for them, and re-layouts, on_device(): lax.all_to_all(out_store[0], DP, split_axis=2, concat_axis=0, tiled=True)  17.8 us
    all_to_all x2, starting transfers between devices, from_everyone(): lax.all_to_all(jnp.broadcast_to(value[None], (count, *value.shape)), axis...  15.9 us
    dot_general x1, matrix products, on_device(): jnp.einsum('qfd,qkd->qkf', precond, right_rows, preferred_element_type=jn...  14.6 us
  transfers between devices with their start and end apart: 6, of which 3 were waited for; matrix products, arithmetic and copies ran while one was open for 25% of the time, Pallas kernels for 0%

commit v1 on v0

v1 whole, which is shorter than its diff:
```python
import jax
import jax.numpy as jnp
import numpy as np
from jax import lax
from jax.experimental import pallas as pl
from jax.experimental.pallas import tpu as pltpu
from jax.sharding import Mesh
from jax.sharding import PartitionSpec as P


NQ = 4
TQ = 32
WIN = 6
R = 32
SPAN = 128
Y, Z, X = "dp_0", "dp_1", "dp_2"
DP = (Y, Z, X)
LAYER = ("layer_0", "layer_1")
LANES = 128
PER_Q = WIN * R

damping = 0.1


def shifted(value, axis, step):
    count = lax.axis_size(axis)
    return lax.ppermute(value, axis, [(i, (i + step) % count) for i in range(count)])


def far_of(before, after, axis):
    half = before.shape[0] // 2
    low = shifted(before[:half], axis, 1)
    high = shifted(after[half:], axis, -1)
    return jnp.concatenate([low, high], axis=0)


def orders(y, z, x, core):
    ring = np.array([0, 3, 1, 2], np.int32)
    pair = np.array([0, 1], np.int32)
    ys, xs = (y + ring) % 4, (x + ring) % 4
    turn = ys[None, :, None] * 8 + ((z + pair) % 2)[None, None, :] * 4 + xs[:, None, None]
    inner = (((core + pair) % 2)[:, None] * 4 + xs[None, :]).reshape(1, 8)
    maps = jnp.concatenate([jnp.broadcast_to(inner, (4, 8)), ys[:, None]], axis=1).reshape(-1)
    own = jnp.where(core == z, 1, 0).reshape(1)
    return turn.reshape(-1).astype(jnp.int32), jnp.concatenate([maps, own]).astype(jnp.int32)


def received(value):
    return lax.ppermute(value, ("layer_1", Z), [(1, 2), (2, 1)])


def traded(value):
    same = lax.axis_index("layer_1") == lax.axis_index(Z)
    return jnp.where(same, value, received(value))


def pack_first(counts, in_acts, in_store):
    rows, width = in_store.shape
    t = in_acts.shape[0]
    count = width // LANES
    step = 8

    def body(counts_ref, acts_ref, store_ref, out_ref):
        row = lax.broadcasted_iota(jnp.int32, (rows, LANES), 0)
        start = (row % R) * SPAN
        alive = start < jnp.where(row < R, counts_ref[0], counts_ref[1])
        for j in range(step):
            out_ref[j, :t, :] = acts_ref[...]
            part = store_ref[:, j * LANES : (j + 1) * LANES].astype(jnp.float32)
            out_ref[j, t:, :] = jnp.where(alive, part, 0.0).astype(jnp.bfloat16)

    return pl.pallas_call(
        body,
        grid_spec=pltpu.PrefetchScalarGridSpec(
            num_scalar_prefetch=1,
            grid=(count // step,),
            in_specs=[
                pl.BlockSpec((t, LANES), lambda i, c: (0, 0)),
                pl.BlockSpec((rows, step * LANES), lambda i, c: (0, i)),
            ],
            out_specs=pl.BlockSpec((step, t + rows, LANES), lambda i, c: (i, 0, 0)),
        ),
        out_shape=jax.ShapeDtypeStruct((count, t + rows, LANES), jnp.bfloat16),
        name="pack_first",
    )(counts, in_acts, in_store)


def pack_left(store, width):
    rows, full = store.shape
    count = full // width
    step = 4

    def body(store_ref, out_ref):
        for j in range(step):
            out_ref[j] = store_ref[:, j * width : (j + 1) * width]

    return pl.pallas_call(
        body,
        grid=(count // step,),
        in_specs=[pl.BlockSpec((rows, step * width), lambda i: (0, i))],
        out_specs=pl.BlockSpec((step, rows, width), lambda i: (i, 0, 0)),
        out_shape=jax.ShapeDtypeStruct((count, rows, width), jnp.bfloat16),
        name="pack_left",
    )(store)


def head(winners, first, basis, t):
    sources, _, lanes = first.shape
    count = winners.shape[0]

    def body(winners_ref, first_ref, basis_ref, out_ref):
        for i in range(count):
            n = winners_ref[i]
            at = pl.multiple_of(t + n % 2 * R, R)
            out_ref[i * R : (i + 1) * R, :] = first_ref[n // 2, pl.ds(at, R), :]
        turned = jnp.zeros((t, lanes), jnp.float32)
        for s in range(0, sources, 2):
            acts = jnp.concatenate([first_ref[s, :t, :], first_ref[s + 1, :t, :]], axis=1)
            turned += jnp.dot(
                acts,
                basis_ref[s * lanes : (s + 2) * lanes, :],
                preferred_element_type=jnp.float32,
            )
        out_ref[count * R :, :] = turned.astype(jnp.bfloat16)

    return pl.pallas_call(
        body,
        grid_spec=pltpu.PrefetchScalarGridSpec(
            num_scalar_prefetch=1,
            grid=(1,),
            in_specs=[
                pl.BlockSpec(first.shape, lambda i, w: (0, 0, 0)),
                pl.BlockSpec(basis.shape, lambda i, w: (0, 0)),
            ],
            out_specs=pl.BlockSpec((count * R + t, lanes), lambda i, w: (0, 0)),
        ),
        out_shape=jax.ShapeDtypeStruct((count * R + t, lanes), jnp.bfloat16),
        name="head",
    )(winners, first, basis)


def turn_part(group, value, order, basis, total):
    blocks, rows, width = value.shape
    out_width = basis.shape[1]
    step = 4
    final = group == 3

    def body(order_ref, value_ref, *refs):
        basis_refs, rest = refs[:step], refs[step:]
        out_ref, sum_ref = rest[-2:]

        @pl.when(pl.program_id(0) == 0)
        def _():
            sum_ref[...] = rest[0][...] if total is not None else jnp.zeros_like(sum_ref)

        part = sum_ref[...]
        for j in range(step):
            part = part + jnp.dot(
                value_ref[j], basis_refs[j][...], preferred_element_type=jnp.float32
            )
        sum_ref[...] = part

        @pl.when(pl.program_id(0) == blocks // step - 1)
        def _():
            out_ref[...] = part.astype(out_ref.dtype)

    whole = pl.BlockSpec((rows, out_width), lambda i, o: (0, 0))
    return pl.pallas_call(
        body,
        grid_spec=pltpu.PrefetchScalarGridSpec(
            num_scalar_prefetch=1,
            grid=(blocks // step,),
            in_specs=[pl.BlockSpec((step, rows, width), lambda i, o: (i, 0, 0))]
            + [
                pl.BlockSpec(
                    (width, out_width), lambda i, o, j=j: (o[group * blocks + i * step + j], 0)
                )
                for j in range(step)
            ]
            + ([] if total is None else [whole]),
            out_specs=whole,
            scratch_shapes=[pltpu.VMEM((rows, out_width), jnp.float32)],
        ),
        out_shape=jax.ShapeDtypeStruct((rows, out_width), jnp.bfloat16 if final else jnp.float32),
        cost_estimate=pl.CostEstimate(
            flops=2 * blocks * width * rows * out_width,
            bytes_accessed=2 * blocks * width * out_width,
            transcendentals=0,
        ),
        name="turn_part",
    )(order, value, *[basis] * step, *([] if total is None else [total]))


def map_part(group, parts, order, eigens, left, total, left_rows):
    blocks = parts[0].shape[0]
    out_width = eigens[0].shape[0]
    count = 2 * blocks
    columns = count * LANES
    base = group * (count + 1)
    own_at = 4 * (count + 1)
    tile = 256
    final = group == 3

    def body(order_ref, near_ref, far_ref, own_ref, got_ref, left_ref, *refs):
        out_ref = refs[-1]

        def rows_of(start, size):
            pieces = [r[b, start : start + size, :] for r in (near_ref, far_ref) for b in range(blocks)]
            return jnp.concatenate(pieces, axis=1)

        def eigen_of(b):
            at = pl.multiple_of(order_ref[base + b] * LANES, LANES)
            own, got = (r[:, pl.ds(at, LANES)].astype(jnp.float32) for r in (own_ref, got_ref))
            return jnp.where(order_ref[own_at] == 1, own, got)

        scale = jnp.concatenate([eigen_of(b) for b in range(count)], axis=1)
        scale = 1.0 / (scale + damping)
        for q in range(NQ):
            product = lax.dot_general(
                left_ref[q * TQ : (q + 1) * TQ, :],
                rows_of(NQ * PER_Q + q * TQ, TQ),
                (((0,), (0,)), ((), ())),
                preferred_element_type=jnp.float32,
            )
            precond = (product * scale).astype(jnp.bfloat16)
            mapped = lax.dot_general(
                precond,
                rows_of(q * PER_Q, PER_Q),
                (((1,), (1,)), ((), ())),
                preferred_element_type=jnp.float32,
            )
            if total is not None:
                mapped = mapped + refs[0][q]
            if final:
                terms = jnp.sum(mapped * refs[1][q].astype(jnp.float32), axis=0, keepdims=True)

                @pl.when(pl.program_id(0) == 0)
                def _():
                    out_ref[q : q + 1, :] = terms

                @pl.when(pl.program_id(0) != 0)
                def _():
                    out_ref[q : q + 1, :] += terms
            else:
                out_ref[q] = mapped

    def own_at_step(i, o):
        return i * o[own_at], o[base + count] * o[own_at]

    def got_at_step(i, o):
        return i * (1 - o[own_at]), 0

    tall = pl.BlockSpec((NQ, tile, PER_Q), lambda i, o: (0, i, 0))
    in_specs = [pl.BlockSpec(p.shape, lambda i, o: (0, 0, 0)) for p in parts]
    in_specs += [
        pl.BlockSpec((tile, columns), own_at_step),
        pl.BlockSpec((tile, columns), got_at_step),
        pl.BlockSpec((NQ * TQ, tile), lambda i, o: (0, i)),
    ]
    operands = [*parts, *eigens, left]
    if total is not None:
        in_specs.append(tall)
        operands.append(total)
    if final:
        in_specs.append(tall)
        operands.append(left_rows)
        out_shape = jax.ShapeDtypeStruct((NQ, PER_Q), jnp.float32)
        out_spec = pl.BlockSpec((NQ, PER_Q), lambda i, o: (0, 0))
    else:
        out_shape = jax.ShapeDtypeStruct((NQ, out_width, PER_Q), jnp.float32)
        out_spec = tall
    return pl.pallas_call(
        body,
        grid_spec=pltpu.PrefetchScalarGridSpec(
            num_scalar_prefetch=1,
            grid=(out_width // tile,),
            in_specs=in_specs,
            out_specs=out_spec,
        ),
        out_shape=out_shape,
        cost_estimate=pl.CostEstimate(
            flops=2 * NQ * out_width * columns * (PER_Q + 8 * TQ),
            bytes_accessed=2 * out_width * columns,
            transcendentals=0,
        ),
        name="map_part",
    )(order, *operands)


def sum_everywhere(value):
    for axis in ("layer_1", Z, "layer_0", Y, X):
        if lax.axis_size(axis) == 2:
            value = value + shifted(value, axis, 1)
        else:
            far, before, after = (shifted(value, axis, step) for step in (2, 1, 3))
            value = (value + far) + (before + after)
    return value


def on_device(
    out_grads, in_acts, out_basis, in_basis, eigenvalues, out_store, in_store, counts, winners
):
    y, z, x = (lax.axis_index(a) for a in DP)
    out_width = out_basis.shape[2]
    out_full = out_basis.shape[1]
    in_full = in_basis.shape[1]
    t = out_grads.shape[1]
    chosen = winners.reshape(NQ * WIN)

    turn_order, map_order = orders(y, z, x, lax.axis_index("layer_1"))

    own = eigenvalues[0]
    quarter = in_full // 4
    got = []
    for group in range(4):
        part = lax.dynamic_slice_in_dim(own, map_order[9 * group + 8] * quarter, quarter, 1)
        got.append(received(part))

    packed = pack_first(counts, in_acts[0], in_store[0].reshape(-1, in_full))
    first = lax.all_to_all(packed, DP, 0, 0, tiled=True)

    grads = out_grads[0]
    grads = jnp.stack([grads, shifted(grads, Z, 1)])
    g_before, g_after = shifted(grads, Y, 1), shifted(grads, Y, -1)
    g_far = far_of(g_before, g_after, Y)
    grads = jnp.concatenate([grads, g_before, g_after, g_far], axis=0)
    g_before, g_after = shifted(grads, X, 1), shifted(grads, X, -1)
    total = turn_part(0, grads, turn_order, out_basis[0], None)
    g_far = far_of(g_before, g_after, X)
    total = turn_part(1, g_before, turn_order, out_basis[0], total)
    total = turn_part(2, g_after, turn_order, out_basis[0], total)
    left = traded(turn_part(3, g_far, turn_order, out_basis[0], total))

    both = head(chosen, first, in_basis[0], t)
    both = traded(both)
    both = [both, *(shifted(both, X, s) for s in (1, -1, 2))]
    both = jnp.stack(both)
    b_before, b_after = shifted(both, Y, 1), shifted(both, Y, -1)
    b_far = far_of(b_before, b_after, Y)

    store = pack_left(out_store[0].reshape(-1, out_full), out_width)
    slices = lax.all_to_all(store, DP, 0, 0, tiled=True)
    left_rows = jnp.take(slices.reshape(-1, R, out_width), chosen, axis=0)
    left_rows = traded(left_rows.reshape(NQ, PER_Q, out_width).transpose(0, 2, 1))

    mapped = None
    for group, part in enumerate((both, b_before, b_after, b_far)):
        parts = (part, shifted(part, "layer_1", 1))
        mapped = map_part(group, parts, map_order, (own, got[group]), left, mapped, left_rows)
    totals = sum_everywhere(mapped.reshape(-1, LANES))
    return totals.reshape(NQ, WIN, R)


def solution(mesh):
    torus = Mesh(
        mesh.devices.reshape(2, 2, 4, 2, 4), ("layer_0", "layer_1", "dp_0", "dp_1", "dp_2")
    )
    return jax.shard_map(
        on_device,
        mesh=torus,
        in_specs=(
            P(LAYER, None, DP),
            P(LAYER, None, DP),
            P(LAYER, None, DP),
            P(LAYER, None, DP),
            P(LAYER, DP, None),
            P(LAYER, DP, None, None),
            P(LAYER, DP, None, None),
            P(DP),
            P(),
        ),
        out_specs=P(),
        check_vma=False,
    )
```

time: 422 us -> 239 us (0.57)
  waiting for transfers between devices: 196 us -> 72.2 us
  local copies, waits for them, and re-layouts: 97.6 us -> 27.1 us
  Pallas kernels: 0 us -> 59.4 us
  blocking collectives: 47.6 us -> 0 us
  starting transfers between devices: 24.3 us -> 68.2 us
  matrix products: 25.7 us -> 0 us
  between operations: 13.2 us -> 2.9 us
  other arithmetic: 15.5 us -> 7.16 us
    all_to_all x3 -> x2, waiting for transfers between devices: 171 us -> 0.01 us  [the longest x1 0.01 us: on_device(): slices = lax.all_to_all(store, DP, 0, 0, tiled=True)]
    ppermute x0 -> x36, waiting for transfers between devices: none -> 72.2 us  [the longest x29 72.2 us: shifted(): lax.ppermute(value, axis, [(i, (i + step) % count) for i in range(count)])]
    pallas_call x0 -> x11, Pallas kernels: none -> 59.4 us  [the longest x4 28.5 us: map_part(): pl.pallas_call(body, grid_spec=pltpu.PrefetchScalarGridSpec(num_scalar_pr...]
    ppermute x0 -> x36, starting transfers between devices: none -> 51.4 us  [the longest x29 42.7 us: shifted(): lax.ppermute(value, axis, [(i, (i + step) % count) for i in range(count)])]
    unnamed x12 -> x26, local copies, waits for them, and re-layouts: 50.9 us -> 6.54 us
    psum x5 -> x0, blocking collectives: 39.6 us -> none  [over_axes(): return functools.reduce(lax.psum, axes, value)]
    dot_general x3 -> x0, matrix products: 25.7 us -> none  [the longest x1 14.6 us: on_device(): jnp.einsum('qfd,qkd->qkf', precond, right_rows, preferred_element_type=jn...]
    all_gather x3 -> x0, waiting for transfers between devices: 24.9 us -> none  [the longest x2 24.9 us: all_blocks(): blocks = lax.all_gather(blocks, axes[k], axis=0, tiled=True)]
  transfers between devices with their start and end apart: 6 -> 38, of which waited for: 3 -> 13; matrix products, arithmetic and copies ran while one was open for 25% -> 13% of each run, Pallas kernels for 0% -> 20%
where the time goes in v1:
time: 239 us; the launch traced here: 237 us
  waiting for transfers between devices  72.2 us (30%)
  starting transfers between devices  68.2 us (29%)
  Pallas kernels  59.4 us (25%)
  local copies, waits for them, and re-layouts  27.1 us (11%)
  other arithmetic  7.16 us (3%)
  between operations  2.9 us (1%)
    ppermute x29, waiting for transfers between devices, shifted(): lax.ppermute(value, axis, [(i, (i + step) % count) for i in range(count)])  72.2 us
    ppermute x29, starting transfers between devices, shifted(): lax.ppermute(value, axis, [(i, (i + step) % count) for i in range(count)])  42.7 us
    pallas_call x4, Pallas kernels, map_part(): pl.pallas_call(body, grid_spec=pltpu.PrefetchScalarGridSpec(num_scalar_pr...  28.5 us
    pallas_call x4, Pallas kernels, turn_part(): pl.pallas_call(body, grid_spec=pltpu.PrefetchScalarGridSpec(num_scalar_pr...  17.6 us
    all_to_all x1, starting transfers between devices, on_device(): first = lax.all_to_all(packed, DP, 0, 0, tiled=True)  9.03 us
    ppermute x7, starting transfers between devices, received(): return lax.ppermute(value, ('layer_1', Z), [(1, 2), (2, 1)])  8.7 us
    all_to_all x1, starting transfers between devices, on_device(): slices = lax.all_to_all(store, DP, 0, 0, tiled=True)  7.79 us
    unnamed x26, local copies, waits for them, and re-layouts  6.54 us
  transfers between devices with their start and end apart: 38, of which 13 were waited for; matrix products, arithmetic and copies ran while one was open for 13% of the time, Pallas kernels for 20%

profile of v1, /device:TPU:8, one launch (start us, length us, event | category | flops | bytes accessed | tf_op | source)
XLA Modules:
  0.0 237.1 jit_solution(14591335759682084398)
XLA Ops:
  0.0 4.1 %pack_first.1 = bf16[32,192,128]{2,1,0:T(8,128)(2,1)} custom-call(s32[2]{0:T(128)} %counts_ref.1, bf16[128,128]{1,0:T(8,128)(2,1)} %bitcast.65, bf16[64,4096]{1,0:T(8,128)(2,1)} %bitcast.59), custom_call_target="tpu_custom_call" | custom-call | tf_op jit(solution)/shard_map/pack_first/pallas_call | solution.py:72
  4.1 9.0 %all-to-all-start = ((bf16[32,192,128]{2,1,0:T(8,128)(2,1)}), bf16[32,192,128]{2,1,0:T(8,128)(2,1)S(1)}, u32[]{:S(2)}, u32[]{:S(2)}) async-start(bf16[32,192,128]{2,1,0:T(8,128)(2,1)} %pack_first.1), calls=%async_computation | async-start | bytes 3145728 | tf_op jit(solution)/shard_map/all_to_all | solution.py:320
  13.2 1.5 collective-permute-start.10
  15.4 19.1 %collective-permute-done.10 = bf16[128,512]{1,0:T(8,128)(2,1)S(1)} collective-permute-done((bf16[128,512]{1,0:T(8,128)(2,1)S(1)}, bf16[128,512]{1,0:T(8,128)(2,1)S(1)}, u32[]{:S(2)}, u32[]{:S(2)}) %collective-permute-start.10) | collective-permute-done | bytes 131104 | tf_op jit(solution)/shard_map/ppermute | solution.py:27
  34.5 1.5 collective-permute-start.11
  38.0 5.6 %pack_left.1 = bf16[32,64,512]{2,1,0:T(8,128)(2,1)} custom-call(bf16[64,16384]{1,0:T(8,128)(2,1)} %bitcast.56), custom_call_target="tpu_custom_call" | custom-call | tf_op jit(solution)/shard_map/pack_left/pallas_call | solution.py:97
  44.3 1.5 collective-permute-start.13
  46.4 7.8 %all-to-all-start.1 = ((bf16[32,64,512]{2,1,0:T(8,128)(2,1)}), bf16[32,64,512]{2,1,0:T(8,128)(2,1)}, u32[]{:S(2)}, u32[]{:S(2)}) async-start(bf16[32,64,512]{2,1,0:T(8,128)(2,1)} %pack_left.1), calls=%async_computation.1 | async-start | bytes 4194304 | tf_op jit(solution)/shard_map/all_to_all | solution.py:342
  54.2 0.7 constant_dynamic-update-slice_fusion.5
  55.0 0.7 constant_dynamic-update-slice_fusion.4
  55.7 3.5 %head.1 = bf16[896,128]{1,0:T(8,128)(2,1)} custom-call(s32[24]{0:T(128)} %reshape.130.winners_ref, bf16[32,192,128]{2,1,0:T(8,128)(2,1)} %copy-done, bf16[4096,128]{1,0:T(8,128)(2,1)} %bitcast.57), custom_call_target="tpu_custom_call" | custom-call | tf_op jit(solution)/shard_map/head/pallas_call | solution.py:126
  61.2 1.5 collective-permute-start.15
  62.7 1.8 collective-permute-start.17
  64.5 1.0 broadcast_select_fusion.1
  65.8 0.7 fusion.7
  69.0 3.1 %collective-permute-start.2 = (bf16[896,128]{1,0:T(8,128)(2,1)S(1)}, bf16[896,128]{1,0:T(8,128)(2,1)S(1)}, u32[]{:S(2)}, u32[]{:S(2)}) collective-permute-start(bf16[896,128]{1,0:T(8,128)(2,1)S(1)} %broadcast_select_fusion.1), channel_id=1, source_target_pairs={{0,3},{1,0},{2,1},{3,2},{4,7},{5,4},{6,5},{7,6},{8,11},{9,8},{10,9... | collective-permute-start | bytes 688136 | tf_op jit(solution)/shard_map/ppermute | solution.py:27
  72.6 4.3 %dynamic-slice_bitcast_fusion = (bf16[512,1024]{1,0:T(8,128)(2,1)}, bf16[512,1024]{1,0:T(8,128)(2,1)}, bf16[512,1024]{1,0:T(8,128)(2,1)}, bf16[512,1024]{1,0:T(8,128)(2,1)}) fusion(bf16[1,512,4096]{2,1,0:T(8,128)(2,1)} %param.15, s32[]{:T(128)S(6)} %select_n.95, s32[]{:T(128)S(6)} %select_n.93, s32[]{:T(128)S(6)} %select_n.89, s32[]{:T(128)S(6)} %select_n.94), kind=kLoop, calls=%fused_computation.3 | loop fusion | bytes 8388624 | tf_op jit(solution)/shard_map/dynamic_slice | solution.py:316
  77.0 31.0 %collective-permute-done.1 = bf16[896,128]{1,0:T(8,128)(2,1)S(1)} collective-permute-done((bf16[896,128]{1,0:T(8,128)(2,1)S(1)}, bf16[896,128]{1,0:T(8,128)(2,1)S(1)}, u32[]{:S(2)}, u32[]{:S(2)}) %collective-permute-start.1) | collective-permute-done | bytes 229408 | tf_op jit(solution)/shard_map/ppermute | solution.py:27
  107.9 1.6 collective-permute-start.25
  109.6 1.4 collective-permute-done.3
  111.1 1.5 collective-permute-start.4
  113.3 0.9 slice.46
  115.0 1.7 collective-permute-start.23
  116.8 2.2 gather_fusion
  119.5 2.7 %collective-permute-start.18 = (bf16[4,128,512]{2,1,0:T(8,128)(2,1)S(1)}, bf16[4,128,512]{2,1,0:T(8,128)(2,1)}, u32[]{:S(2)}, u32[]{:S(2)}) collective-permute-start(bf16[4,128,512]{2,1,0:T(8,128)(2,1)S(1)} %slice.47), channel_id=1, source_target_pairs={{0,3},{1,0},{2,1},{3,2},{4,7},{5,4},{6,5},{7,6},{8,11},{9,8},{10,9... | collective-permute-start | bytes 1572872 | tf_op jit(solution)/shard_map/ppermute | solution.py:27
  122.4 1.3 copy.18
  123.6 5.8 %collective-permute-done.16 = bf16[4,128,512]{2,1,0:T(8,128)(2,1)} collective-permute-done((bf16[4,128,512]{2,1,0:T(8,128)(2,1)}, bf16[4,128,512]{2,1,0:T(8,128)(2,1)}, u32[]{:S(2)}, u32[]{:S(2)}) %collective-permute-start.16) | collective-permute-done | bytes 524320 | tf_op jit(solution)/shard_map/ppermute | solution.py:27
  129.5 4.5 %collective-permute-done.4.near_ref = bf16[4,896,128]{2,1,0:T(8,128)(2,1)} collective-permute-done((bf16[4,896,128]{2,1,0:T(8,128)(2,1)S(1)}, bf16[4,896,128]{2,1,0:T(8,128)(2,1)}, u32[]{:S(2)}, u32[]{:S(2)}) %collective-permute-start.4) | collective-permute-done | bytes 917536 | tf_op jit(solution)/shard_map/ppermute | solution.py:27
  134.0 1.5 collective-permute-start.26
  136.2 1.8 slice.42
  138.0 1.6 collective-permute-start.5
  139.6 4.3 %turn_part.4.refs_4_ = f32[128,512]{1,0:T(8,128)} custom-call(s32[32]{0:T(128)} %add.177.order_ref, bf16[8,128,512]{2,1,0:T(8,128)(2,1)} %constant_dynamic-update-slice_fusion.2.value_ref, bf16[16384,512]{1,0:T(8,128)(2,1)} %bitcast.35, bf16[16384,512]{1,0:T(8,128)(2,1)} %bitcast.36, bf16[16384,512]{1,0:T(8,128)(2,1)} %bitcast.37, bf16[16384,512]{1,0:T(8,128)(2,1)} %bitcast.38), custom_call_target="tpu_custom_call" | custom-call | flops 536870912 | bytes 4194304 | tf_op jit(solution)/shard_map/turn_part/pallas_call | solution.py:168
  143.9 4.5 %turn_part.5.refs_4_ = f32[128,512]{1,0:T(8,128)} custom-call(s32[32]{0:T(128)} %add.177.order_ref, bf16[8,128,512]{2,1,0:T(8,128)(2,1)} %copy-done.3, bf16[16384,512]{1,0:T(8,128)(2,1)} %bitcast.39, bf16[16384,512]{1,0:T(8,128)(2,1)} %bitcast.40, bf16[16384,512]{1,0:T(8,128)(2,1)} %bitcast.41, bf16[16384,512]{1,0:T(8,128)(2,1)} %bitcast.42, ...), custom_call_target="tpu_custom_call" | custom-call | flops 536870912 | bytes 4194304 | tf_op jit(solution)/shard_map/turn_part/pallas_call | solution.py:168
  148.4 1.8 slice.43
  150.7 4.4 %turn_part.6.refs_4_ = f32[128,512]{1,0:T(8,128)} custom-call(s32[32]{0:T(128)} %add.177.order_ref, bf16[8,128,512]{2,1,0:T(8,128)(2,1)} %copy-done.2, bf16[16384,512]{1,0:T(8,128)(2,1)} %bitcast.43, bf16[16384,512]{1,0:T(8,128)(2,1)} %bitcast.44, bf16[16384,512]{1,0:T(8,128)(2,1)} %bitcast.45, bf16[16384,512]{1,0:T(8,128)(2,1)} %bitcast.46, ...), custom_call_target="tpu_custom_call" | custom-call | flops 536870912 | bytes 4194304 | tf_op jit(solution)/shard_map/turn_part/pallas_call | solution.py:168
  155.1 2.3 pad_maximum_fusion.value_ref
  157.4 4.4 %turn_part.7 = bf16[128,512]{1,0:T(8,128)(2,1)} custom-call(s32[32]{0:T(128)} %add.177.order_ref, bf16[8,128,512]{2,1,0:T(8,128)(2,1)} %pad_maximum_fusion.value_ref, bf16[16384,512]{1,0:T(8,128)(2,1)} %bitcast.47, bf16[16384,512]{1,0:T(8,128)(2,1)} %bitcast.48, bf16[16384,512]{1,0:T(8,128)(2,1)} %bitcast.49, bf16[16384,512]{1,0:T(8,128)(2,1)} %bitcast.50, ...), custom_call_target="tpu_custom_call" | custom-call | flops 536870912 | bytes 4194304 | tf_op jit(solution)/shard_map/turn_part/pallas_call | solution.py:168
  163.1 0.9 collective-permute-start.21
  164.0 8.2 %collective-permute-start.22 = (bf16[4,896,128]{2,1,0:T(8,128)(2,1)}, bf16[4,896,128]{2,1,0:T(8,128)(2,1)}, u32[]{:S(2)}, u32[]{:S(2)}) collective-permute-start(bf16[4,896,128]{2,1,0:T(8,128)(2,1)} %collective-permute-done.4.near_ref), channel_id=1, source_target_pairs={{0,32},{32,0},{1,33},{33,1},{2,34},{34,2},{3,35},{35,3},{4,36},{36... | collective-permute-start | bytes 2752520 | tf_op jit(solution)/shard_map/ppermute | solution.py:27
  172.2 1.8 constant_dynamic-update-slice_fusion.1
  174.0 1.8 constant_dynamic-update-slice_fusion.near_ref
  175.9 1.6 collective-permute-start.9
  177.5 0.9 collective-permute-start.8
  178.4 1.6 broadcast_select_fusion.2.left_ref
  179.9 1.4 copy.19
  181.4 1.1 broadcast_select_fusion.refs_1_
  182.5 6.5 %map_part.4.refs_0_ = f32[4,512,192]{2,1,0:T(8,128)} custom-call(s32[37]{0:T(128)} %pad_add_fusion.1.order_ref, bf16[4,896,128]{2,1,0:T(8,128)(2,1)} %copy-done.1, bf16[4,896,128]{2,1,0:T(8,128)(2,1)} %collective-permute-done.24.far_ref, bf16[512,4096]{1,0:T(8,128)(2,1)} %bitcast.51, bf16[512,1024]{1,0:T(8,128)(2,1)} %collective-permute-done.25.got_ref, ...), custom_call_target="tpu_custom_call" | custom-call | flops 1879048192 | bytes 1048576 | tf_op jit(solution)/shard_map/map_part/pallas_call | solution.py:272
  189.0 6.8 %map_part.5.refs_0_ = f32[4,512,192]{2,1,0:T(8,128)} custom-call(s32[37]{0:T(128)} %pad_add_fusion.1.order_ref, bf16[4,896,128]{2,1,0:T(8,128)(2,1)} %collective-permute-done.4.near_ref, bf16[4,896,128]{2,1,0:T(8,128)(2,1)} %collective-permute-done.22.far_ref, bf16[512,4096]{1,0:T(8,128)(2,1)} %bitcast.52, ...), custom_call_target="tpu_custom_call" | custom-call | flops 1879048192 | bytes 1048576 | tf_op jit(solution)/shard_map/map_part/pallas_call | solution.py:272
  195.8 1.0 copy-done.4
  196.8 6.9 %map_part.6.refs_0_ = f32[4,512,192]{2,1,0:T(8,128)} custom-call(s32[37]{0:T(128)} %pad_add_fusion.1.order_ref, bf16[4,896,128]{2,1,0:T(8,128)(2,1)} %collective-permute-done.6.near_ref, bf16[4,896,128]{2,1,0:T(8,128)(2,1)} %collective-permute-done.20.far_ref, bf16[512,4096]{1,0:T(8,128)(2,1)} %bitcast.53, bf16[512,1024]{1,0:T(8,128)(2,1)} %copy-done.4, ...), custom_call_target="tpu_custom_call" | custom-call | flops 1879048192 | bytes 1048576 | tf_op jit(solution)/shard_map/map_part/pallas_call | solution.py:272
  203.6 8.4 %map_part.7 = f32[4,192]{1,0:T(4,128)} custom-call(s32[37]{0:T(128)} %pad_add_fusion.1.order_ref, bf16[4,896,128]{2,1,0:T(8,128)(2,1)} %constant_dynamic-update-slice_fusion.near_ref, bf16[4,896,128]{2,1,0:T(8,128)(2,1)} %collective-permute-done.8.far_ref, bf16[512,4096]{1,0:T(8,128)(2,1)} %bitcast.54, bf16[512,1024]{1,0:T(8,128)(2,1)} %collective-permute-done.9.got_ref, ...), custom_call_target="tpu_custom_call" | custom-call | flops 1879048192 | bytes 1048576 | tf_op jit(solution)/shard_map/map_part/pallas_call | solution.py:272
  212.0 0.8 reshape.133
  212.7 1.2 collective-permute-done.27
  213.9 1.8 collective-permute-start.28
  215.7 1.8 collective-permute-done.28
  217.5 3.6 %collective-permute-start.29 = (f32[6,128]{1,0:T(8,128)S(1)}, f32[6,128]{1,0:T(8,128)S(1)}, u32[]{:S(2)}, u32[]{:S(2)}) collective-permute-start(f32[6,128]{1,0:T(8,128)S(1)} %add.184), channel_id=1, source_target_pairs={{0,64},{64,0},{1,65},{65,1},{2,66},{66,2},{3,67},{67,3},{4,68},{68... | collective-permute-start | bytes 9224 | tf_op jit(solution)/shard_map/ppermute | solution.py:27
  221.1 1.6 collective-permute-done.29
  222.7 2.2 collective-permute-start.30
  224.9 2.4 %collective-permute-start.31 = (f32[6,128]{1,0:T(8,128)S(1)}, f32[6,128]{1,0:T(8,128)S(1)}, u32[]{:S(2)}, u32[]{:S(2)}) collective-permute-start(f32[6,128]{1,0:T(8,128)S(1)} %add.185), channel_id=1, source_target_pairs={{0,8},{8,16},{16,24},{24,0},{1,9},{9,17},{17,25},{25,1},{2,10},{10... | collective-permute-start | bytes 9224 | tf_op jit(solution)/shard_map/ppermute | solution.py:27
  227.8 0.8 collective-permute-done.31
  228.6 2.3 collective-permute-done.32
  230.9 1.8 collective-permute-start.34
  232.8 1.5 collective-permute-start.35
  234.2 1.8 collective-permute-done.33
  (97 shorter events, 13.0 us)
Async XLA Ops:
  4.1 9.1 %copy-start.5 = (bf16[1,128,512]{2,1,0:T(8,128)(2,1)S(1)}, bf16[1,128,512]{2,1,0:T(8,128)(2,1)}, u32[]{:S(2)}) copy-start(bf16[1,128,512]{2,1,0:T(8,128)(2,1)} %param.11) | copy-start | bytes 393220
  4.1 10.6 %copy-start.9 = (s32[4]{0:T(128)S(1)}, s32[4]{0:T(128)}, u32[]{:S(2)}) copy-start(s32[4]{0:T(128)} %constant.92.clone) | copy-start | bytes 52
  4.1 33.3 %copy-start.6 = (s32[4,6]{1,0:T(4,128)S(1)}, s32[4,6]{1,0:T(4,128)}, u32[]{:S(2)}) copy-start(s32[4,6]{1,0:T(4,128)} %param.19) | copy-start | bytes 292
  4.1 42.3 %all-to-all-start = ((bf16[32,192,128]{2,1,0:T(8,128)(2,1)}), bf16[32,192,128]{2,1,0:T(8,128)(2,1)S(1)}, u32[]{:S(2)}, u32[]{:S(2)}) async-start(bf16[32,192,128]{2,1,0:T(8,128)(2,1)} %pack_first.1), calls=%async_computation | async-start | bytes 3145728 | tf_op jit(solution)/shard_map/all_to_all | solution.py:320
  13.2 21.3 %collective-permute-start.10 = (bf16[128,512]{1,0:T(8,128)(2,1)S(1)}, bf16[128,512]{1,0:T(8,128)(2,1)S(1)}, u32[]{:S(2)}, u32[]{:S(2)}) collective-permute-start(bf16[128,512]{1,0:T(8,128)(2,1)S(1)} %bitcast.60), channel_id=1, source_target_pairs={{0,4},{4,0},{1,5},{5,1},{2,6},{6,2},{3,7},{7,3},{8,12},{12,8},{9,1... | collective-permute-start | bytes 393224 | tf_op jit(solution)/shard_map/ppermute | solution.py:27
  14.8 0.5 copy-start.7
  34.5 9.7 %collective-permute-start.11 = (bf16[2,128,512]{2,1,0:T(8,128)(2,1)S(1)}, bf16[2,128,512]{2,1,0:T(8,128)(2,1)S(1)}, u32[]{:S(2)}, u32[]{:S(2)}) collective-permute-start(bf16[2,128,512]{2,1,0:T(8,128)(2,1)S(1)} %pad_maximum_fusion.2), channel_id=1, source_target_pairs={{0,8},{8,16},{16,24},{24,0},{1,9},{9,17},{17,25},{25,1},{2,10},{10... | collective-permute-start | bytes 786440 | tf_op jit(solution)/shard_map/ppermute | solution.py:27
  36.1 9.7 %collective-permute-start.12 = (bf16[2,128,512]{2,1,0:T(8,128)(2,1)S(1)}, bf16[2,128,512]{2,1,0:T(8,128)(2,1)S(1)}, u32[]{:S(2)}, u32[]{:S(2)}) collective-permute-start(bf16[2,128,512]{2,1,0:T(8,128)(2,1)S(1)} %pad_maximum_fusion.2), channel_id=1, source_target_pairs={{0,24},{8,0},{16,8},{24,16},{1,25},{9,1},{17,9},{25,17},{2,26},{10... | collective-permute-start | bytes 786440 | tf_op jit(solution)/shard_map/ppermute | solution.py:27
  44.3 15.6 %collective-permute-start.13 = (bf16[1,128,512]{2,1,0:T(8,128)(2,1)S(1)}, bf16[1,128,512]{2,1,0:T(8,128)(2,1)S(1)}, u32[]{:S(2)}, u32[]{:S(2)}) collective-permute-start(bf16[1,128,512]{2,1,0:T(8,128)(2,1)S(1)} %slice.44), channel_id=1, source_target_pairs={{0,8},{8,16},{16,24},{24,0},{1,9},{9,17},{17,25},{25,1},{2,10},{10... | collective-permute-start | bytes 393224 | tf_op jit(solution)/shard_map/ppermute | solution.py:27
  45.8 14.8 %collective-permute-start.14 = (bf16[1,128,512]{2,1,0:T(8,128)(2,1)S(1)}, bf16[1,128,512]{2,1,0:T(8,128)(2,1)S(1)}, u32[]{:S(2)}, u32[]{:S(2)}) collective-permute-start(bf16[1,128,512]{2,1,0:T(8,128)(2,1)S(1)} %slice.45), channel_id=1, source_target_pairs={{0,24},{8,0},{16,8},{24,16},{1,25},{9,1},{17,9},{25,17},{2,26},{10... | collective-permute-start | bytes 393224 | tf_op jit(solution)/shard_map/ppermute | solution.py:27
  46.4 8.5 %copy-start = (bf16[32,192,128]{2,1,0:T(8,128)(2,1)}, bf16[32,192,128]{2,1,0:T(8,128)(2,1)S(1)}, u32[]{:S(2)}) copy-start(bf16[32,192,128]{2,1,0:T(8,128)(2,1)S(1)} %all-to-all-done.first_ref) | copy-start | bytes 4718596
  46.4 70.3 %all-to-all-start.1 = ((bf16[32,64,512]{2,1,0:T(8,128)(2,1)}), bf16[32,64,512]{2,1,0:T(8,128)(2,1)}, u32[]{:S(2)}, u32[]{:S(2)}) async-start(bf16[32,64,512]{2,1,0:T(8,128)(2,1)} %pack_left.1), calls=%async_computation.1 | async-start | bytes 4194304 | tf_op jit(solution)/shard_map/all_to_all | solution.py:342
  59.2 5.2 %collective-permute-start = (bf16[896,128]{1,0:T(8,128)(2,1)}, bf16[896,128]{1,0:T(8,128)(2,1)S(1)}, u32[]{:S(2)}, u32[]{:S(2)}) collective-permute-start(bf16[896,128]{1,0:T(8,128)(2,1)} %head.1), channel_id=1, source_target_pairs={{4,32},{32,4},{5,33},{33,5},{6,34},{34,6},{7,35},{35,7},{12,40},{4... | collective-permute-start | bytes 688136 | tf_op jit(solution)/shard_map/ppermute | solution.py:49
  61.2 52.1 %collective-permute-start.15 = (bf16[8,128,512]{2,1,0:T(8,128)(2,1)}, bf16[8,128,512]{2,1,0:T(8,128)(2,1)S(1)}, u32[]{:S(2)}, u32[]{:S(2)}) collective-permute-start(bf16[8,128,512]{2,1,0:T(8,128)(2,1)} %constant_dynamic-update-slice_fusion.2.value_ref), channel_id=1, source_target_pairs={{0,1},{1,2},{2,3},{3,0},{4,5},{5,6},{6,7},{7,4},{8,9},{9,10},{10,1... | collective-permute-start | bytes 3145736 | tf_op jit(solution)/shard_map/ppermute | solution.py:27
  62.7 52.3 %collective-permute-start.17 = (bf16[8,128,512]{2,1,0:T(8,128)(2,1)}, bf16[8,128,512]{2,1,0:T(8,128)(2,1)S(1)}, u32[]{:S(2)}, u32[]{:S(2)}) collective-permute-start(bf16[8,128,512]{2,1,0:T(8,128)(2,1)} %constant_dynamic-update-slice_fusion.2.value_ref), channel_id=1, source_target_pairs={{0,3},{1,0},{2,1},{3,2},{4,7},{5,4},{6,5},{7,6},{8,11},{9,8},{10,9... | collective-permute-start | bytes 3145736 | tf_op jit(solution)/shard_map/ppermute | solution.py:27
  65.4 42.5 %collective-permute-start.1 = (bf16[896,128]{1,0:T(8,128)(2,1)S(1)}, bf16[896,128]{1,0:T(8,128)(2,1)S(1)}, u32[]{:S(2)}, u32[]{:S(2)}) collective-permute-start(bf16[896,128]{1,0:T(8,128)(2,1)S(1)} %broadcast_select_fusion.1), channel_id=1, source_target_pairs={{0,1},{1,2},{2,3},{3,0},{4,5},{5,6},{6,7},{7,4},{8,9},{9,10},{10,1... | collective-permute-start | bytes 688136 | tf_op jit(solution)/shard_map/ppermute | solution.py:27
  69.0 40.5 %collective-permute-start.2 = (bf16[896,128]{1,0:T(8,128)(2,1)S(1)}, bf16[896,128]{1,0:T(8,128)(2,1)S(1)}, u32[]{:S(2)}, u32[]{:S(2)}) collective-permute-start(bf16[896,128]{1,0:T(8,128)(2,1)S(1)} %broadcast_select_fusion.1), channel_id=1, source_target_pairs={{0,3},{1,0},{2,1},{3,2},{4,7},{5,4},{6,5},{7,6},{8,11},{9,8},{10,9... | collective-permute-start | bytes 688136 | tf_op jit(solution)/shard_map/ppermute | solution.py:27
  72.1 38.9 %collective-permute-start.3 = (bf16[896,128]{1,0:T(8,128)(2,1)S(1)}, bf16[896,128]{1,0:T(8,128)(2,1)S(1)}, u32[]{:S(2)}, u32[]{:S(2)}) collective-permute-start(bf16[896,128]{1,0:T(8,128)(2,1)S(1)} %broadcast_select_fusion.1), channel_id=1, source_target_pairs={{0,2},{1,3},{2,0},{3,1},{4,6},{5,7},{6,4},{7,5},{8,10},{9,11},{10,... | collective-permute-start | bytes 688136 | tf_op jit(solution)/shard_map/ppermute | solution.py:27
  107.9 11.6 %collective-permute-start.25 = (bf16[512,1024]{1,0:T(8,128)(2,1)}, bf16[512,1024]{1,0:T(8,128)(2,1)}, u32[]{:S(2)}, u32[]{:S(2)}) collective-permute-start(bf16[512,1024]{1,0:T(8,128)(2,1)} %get-tuple-element.7), channel_id=1, source_target_pairs={{4,32},{32,4},{5,33},{33,5},{6,34},{34,6},{7,35},{35,7},{12,40},{4... | collective-permute-start | bytes 3145736 | tf_op jit(solution)/shard_map/ppermute | solution.py:49
  111.1 18.4 %copy-start.1 = (bf16[4,896,128]{2,1,0:T(8,128)(2,1)}, bf16[4,896,128]{2,1,0:T(8,128)(2,1)S(1)}, u32[]{:S(2)}) copy-start(bf16[4,896,128]{2,1,0:T(8,128)(2,1)S(1)} %pad_maximum_fusion.1.near_ref) | copy-start | bytes 2752516
  111.1 22.9 %collective-permute-start.4 = (bf16[4,896,128]{2,1,0:T(8,128)(2,1)S(1)}, bf16[4,896,128]{2,1,0:T(8,128)(2,1)}, u32[]{:S(2)}, u32[]{:S(2)}) collective-permute-start(bf16[4,896,128]{2,1,0:T(8,128)(2,1)S(1)} %pad_maximum_fusion.1.near_ref), channel_id=1, source_target_pairs={{0,8},{8,16},{16,24},{24,0},{1,9},{9,17},{17,25},{25,1},{2,10},{10... | collective-permute-start | bytes 2752520 | tf_op jit(solution)/shard_map/ppermute | solution.py:27
  112.7 25.3 %collective-permute-start.6 = (bf16[4,896,128]{2,1,0:T(8,128)(2,1)S(1)}, bf16[4,896,128]{2,1,0:T(8,128)(2,1)}, u32[]{:S(2)}, u32[]{:S(2)}) collective-permute-start(bf16[4,896,128]{2,1,0:T(8,128)(2,1)S(1)} %pad_maximum_fusion.1.near_ref), channel_id=1, source_target_pairs={{0,24},{8,0},{16,8},{24,16},{1,25},{9,1},{17,9},{25,17},{2,26},{10... | collective-permute-start | bytes 2752520 | tf_op jit(solution)/shard_map/ppermute | solution.py:27
  113.3 3.5 %copy-start.3 = (bf16[8,128,512]{2,1,0:T(8,128)(2,1)}, bf16[8,128,512]{2,1,0:T(8,128)(2,1)S(1)}, u32[]{:S(2)}) copy-start(bf16[8,128,512]{2,1,0:T(8,128)(2,1)S(1)} %collective-permute-done.15.value_ref) | copy-start | bytes 3145732
  114.2 15.3 %collective-permute-start.16 = (bf16[4,128,512]{2,1,0:T(8,128)(2,1)}, bf16[4,128,512]{2,1,0:T(8,128)(2,1)}, u32[]{:S(2)}, u32[]{:S(2)}) collective-permute-start(bf16[4,128,512]{2,1,0:T(8,128)(2,1)} %slice.46), channel_id=1, source_target_pairs={{0,1},{1,2},{2,3},{3,0},{4,5},{5,6},{6,7},{7,4},{8,9},{9,10},{10,1... | collective-permute-start | bytes 1572872 | tf_op jit(solution)/shard_map/ppermute | solution.py:27
  115.0 4.0 %copy-start.2 = (bf16[8,128,512]{2,1,0:T(8,128)(2,1)}, bf16[8,128,512]{2,1,0:T(8,128)(2,1)S(1)}, u32[]{:S(2)}) copy-start(bf16[8,128,512]{2,1,0:T(8,128)(2,1)S(1)} %collective-permute-done.17.value_ref) | copy-start | bytes 3145732
  115.0 46.8 %collective-permute-start.23 = (bf16[512,1024]{1,0:T(8,128)(2,1)}, bf16[512,1024]{1,0:T(8,128)(2,1)}, u32[]{:S(2)}, u32[]{:S(2)}) collective-permute-start(bf16[512,1024]{1,0:T(8,128)(2,1)} %get-tuple-element.10), channel_id=1, source_target_pairs={{4,32},{32,4},{5,33},{33,5},{6,34},{34,6},{7,35},{35,7},{12,40},{4... | collective-permute-start | bytes 3145736 | tf_op jit(solution)/shard_map/ppermute | solution.py:49
  119.5 16.0 %copy-start.8 = (s32[4]{0:T(128)S(1)}, s32[4]{0:T(128)}, u32[]{:S(2)}) copy-start(s32[4]{0:T(128)} %copy-done.7) | copy-start | bytes 52
  119.5 30.7 %collective-permute-start.18 = (bf16[4,128,512]{2,1,0:T(8,128)(2,1)S(1)}, bf16[4,128,512]{2,1,0:T(8,128)(2,1)}, u32[]{:S(2)}, u32[]{:S(2)}) collective-permute-start(bf16[4,128,512]{2,1,0:T(8,128)(2,1)S(1)} %slice.47), channel_id=1, source_target_pairs={{0,3},{1,0},{2,1},{3,2},{4,7},{5,4},{6,5},{7,6},{8,11},{9,8},{10,9... | collective-permute-start | bytes 1572872 | tf_op jit(solution)/shard_map/ppermute | solution.py:27
  129.5 48.0 %collective-permute-start.24 = (bf16[4,896,128]{2,1,0:T(8,128)(2,1)S(1)}, bf16[4,896,128]{2,1,0:T(8,128)(2,1)}, u32[]{:S(2)}, u32[]{:S(2)}) collective-permute-start(bf16[4,896,128]{2,1,0:T(8,128)(2,1)S(1)} %pad_maximum_fusion.1.near_ref), channel_id=1, source_target_pairs={{0,32},{32,0},{1,33},{33,1},{2,34},{34,2},{3,35},{35,3},{4,36},{36... | collective-permute-start | bytes 2752520 | tf_op jit(solution)/shard_map/ppermute | solution.py:27
  134.0 41.9 %collective-permute-start.26 = (bf16[4,512,192]{1,2,0:T(8,128)(2,1)}, bf16[4,512,192]{1,2,0:T(8,128)(2,1)}, u32[]{:S(2)}, u32[]{:S(2)}) collective-permute-start(bf16[4,512,192]{1,2,0:T(8,128)(2,1)} %copy.18), channel_id=1, source_target_pairs={{4,32},{32,4},{5,33},{33,5},{6,34},{34,6},{7,35},{35,7},{12,40},{4... | collective-permute-start | bytes 2359304 | tf_op jit(solution)/shard_map/ppermute | solution.py:49
  138.0 26.0 %collective-permute-start.5 = (bf16[2,896,128]{2,1,0:T(8,128)(2,1)}, bf16[2,896,128]{2,1,0:T(8,128)(2,1)}, u32[]{:S(2)}, u32[]{:S(2)}) collective-permute-start(bf16[2,896,128]{2,1,0:T(8,128)(2,1)} %slice.42), channel_id=1, source_target_pairs={{0,8},{8,16},{16,24},{24,0},{1,9},{9,17},{17,25},{25,1},{2,10},{10... | collective-permute-start | bytes 1376264 | tf_op jit(solution)/shard_map/ppermute | solution.py:27
  150.2 23.8 %collective-permute-start.7 = (bf16[2,896,128]{2,1,0:T(8,128)(2,1)}, bf16[2,896,128]{2,1,0:T(8,128)(2,1)}, u32[]{:S(2)}, u32[]{:S(2)}) collective-permute-start(bf16[2,896,128]{2,1,0:T(8,128)(2,1)} %slice.43), channel_id=1, source_target_pairs={{0,24},{8,0},{16,8},{24,16},{1,25},{9,1},{17,9},{25,17},{2,26},{10... | collective-permute-start | bytes 1376264 | tf_op jit(solution)/shard_map/ppermute | solution.py:27
  161.8 1.3 collective-permute-start.19
  163.1 32.7 %collective-permute-start.21 = (bf16[512,1024]{1,0:T(8,128)(2,1)}, bf16[512,1024]{1,0:T(8,128)(2,1)S(1)}, u32[]{:S(2)}, u32[]{:S(2)}) collective-permute-start(bf16[512,1024]{1,0:T(8,128)(2,1)} %get-tuple-element.8), channel_id=1, source_target_pairs={{4,32},{32,4},{5,33},{33,5},{6,34},{34,6},{7,35},{35,7},{12,40},{4... | collective-permute-start | bytes 3145736 | tf_op jit(solution)/shard_map/ppermute | solution.py:49
  164.0 24.9 %collective-permute-start.22 = (bf16[4,896,128]{2,1,0:T(8,128)(2,1)}, bf16[4,896,128]{2,1,0:T(8,128)(2,1)}, u32[]{:S(2)}, u32[]{:S(2)}) collective-permute-start(bf16[4,896,128]{2,1,0:T(8,128)(2,1)} %collective-permute-done.4.near_ref), channel_id=1, source_target_pairs={{0,32},{32,0},{1,33},{33,1},{2,34},{34,2},{3,35},{35,3},{4,36},{36... | collective-permute-start | bytes 2752520 | tf_op jit(solution)/shard_map/ppermute | solution.py:27
  174.0 21.8 %collective-permute-start.20 = (bf16[4,896,128]{2,1,0:T(8,128)(2,1)}, bf16[4,896,128]{2,1,0:T(8,128)(2,1)}, u32[]{:S(2)}, u32[]{:S(2)}) collective-permute-start(bf16[4,896,128]{2,1,0:T(8,128)(2,1)} %collective-permute-done.6.near_ref), channel_id=1, source_target_pairs={{0,32},{32,0},{1,33},{33,1},{2,34},{34,2},{3,35},{35,3},{4,36},{36... | collective-permute-start | bytes 2752520 | tf_op jit(solution)/shard_map/ppermute | solution.py:27
  175.9 27.8 %collective-permute-start.9 = (bf16[512,1024]{1,0:T(8,128)(2,1)}, bf16[512,1024]{1,0:T(8,128)(2,1)}, u32[]{:S(2)}, u32[]{:S(2)}) collective-permute-start(bf16[512,1024]{1,0:T(8,128)(2,1)} %get-tuple-element.9), channel_id=1, source_target_pairs={{4,32},{32,4},{5,33},{33,5},{6,34},{34,6},{7,35},{35,7},{12,40},{4... | collective-permute-start | bytes 3145736 | tf_op jit(solution)/shard_map/ppermute | solution.py:49
  177.5 26.1 %collective-permute-start.8 = (bf16[4,896,128]{2,1,0:T(8,128)(2,1)}, bf16[4,896,128]{2,1,0:T(8,128)(2,1)}, u32[]{:S(2)}, u32[]{:S(2)}) collective-permute-start(bf16[4,896,128]{2,1,0:T(8,128)(2,1)} %constant_dynamic-update-slice_fusion.near_ref), channel_id=1, source_target_pairs={{0,32},{32,0},{1,33},{33,1},{2,34},{34,2},{3,35},{35,3},{4,36},{36... | collective-permute-start | bytes 2752520 | tf_op jit(solution)/shard_map/ppermute | solution.py:27
  195.8 1.0 copy-start.4
  212.7 1.2 collective-permute-start.27
  213.9 3.6 %collective-permute-start.28 = (f32[6,128]{1,0:T(8,128)S(1)}, f32[6,128]{1,0:T(8,128)S(1)}, u32[]{:S(2)}, u32[]{:S(2)}) collective-permute-start(f32[6,128]{1,0:T(8,128)S(1)} %add.183), channel_id=1, source_target_pairs={{0,4},{4,0},{1,5},{5,1},{2,6},{6,2},{3,7},{7,3},{8,12},{12,8},{9,1... | collective-permute-start | bytes 9224 | tf_op jit(solution)/shard_map/ppermute | solution.py:27
  217.5 5.2 %collective-permute-start.29 = (f32[6,128]{1,0:T(8,128)S(1)}, f32[6,128]{1,0:T(8,128)S(1)}, u32[]{:S(2)}, u32[]{:S(2)}) collective-permute-start(f32[6,128]{1,0:T(8,128)S(1)} %add.184), channel_id=1, source_target_pairs={{0,64},{64,0},{1,65},{65,1},{2,66},{66,2},{3,67},{67,3},{4,68},{68... | collective-permute-start | bytes 9224 | tf_op jit(solution)/shard_map/ppermute | solution.py:27
  222.7 5.1 %collective-permute-start.30 = (f32[6,128]{1,0:T(8,128)S(1)}, f32[6,128]{1,0:T(8,128)S(1)}, u32[]{:S(2)}, u32[]{:S(2)}) collective-permute-start(f32[6,128]{1,0:T(8,128)S(1)} %add.185), channel_id=1, source_target_pairs={{0,16},{8,24},{16,0},{24,8},{1,17},{9,25},{17,1},{25,9},{2,18},{10... | collective-permute-start | bytes 9224 | tf_op jit(solution)/shard_map/ppermute | solution.py:27
  224.9 3.7 %collective-permute-start.31 = (f32[6,128]{1,0:T(8,128)S(1)}, f32[6,128]{1,0:T(8,128)S(1)}, u32[]{:S(2)}, u32[]{:S(2)}) collective-permute-start(f32[6,128]{1,0:T(8,128)S(1)} %add.185), channel_id=1, source_target_pairs={{0,8},{8,16},{16,24},{24,0},{1,9},{9,17},{17,25},{25,1},{2,10},{10... | collective-permute-start | bytes 9224 | tf_op jit(solution)/shard_map/ppermute | solution.py:27
  227.3 3.6 %collective-permute-start.32 = (f32[6,128]{1,0:T(8,128)S(1)}, f32[6,128]{1,0:T(8,128)S(1)}, u32[]{:S(2)}, u32[]{:S(2)}) collective-permute-start(f32[6,128]{1,0:T(8,128)S(1)} %add.185), channel_id=1, source_target_pairs={{0,24},{8,0},{16,8},{24,16},{1,25},{9,1},{17,9},{25,17},{2,26},{10... | collective-permute-start | bytes 9224 | tf_op jit(solution)/shard_map/ppermute | solution.py:27
  230.9 5.1 %collective-permute-start.33 = (f32[6,128]{1,0:T(8,128)S(1)}, f32[6,128]{1,0:T(8,128)S(1)}, u32[]{:S(2)}, u32[]{:S(2)}) collective-permute-start(f32[6,128]{1,0:T(8,128)S(1)} %add_add_fusion.1), channel_id=1, source_target_pairs={{0,2},{1,3},{2,0},{3,1},{4,6},{5,7},{6,4},{7,5},{8,10},{9,11},{10,... | collective-permute-start | bytes 9224 | tf_op jit(solution)/shard_map/ppermute | solution.py:27
  230.9 5.1 %collective-permute-start.34 = (f32[6,128]{1,0:T(8,128)S(1)}, f32[6,128]{1,0:T(8,128)S(1)}, u32[]{:S(2)}, u32[]{:S(2)}) collective-permute-start(f32[6,128]{1,0:T(8,128)S(1)} %add_add_fusion.1), channel_id=1, source_target_pairs={{0,1},{1,2},{2,3},{3,0},{4,5},{5,6},{6,7},{7,4},{8,9},{9,10},{10,1... | collective-permute-start | bytes 9224 | tf_op jit(solution)/shard_map/ppermute | solution.py:27
  232.8 3.6 %collective-permute-start.35 = (f32[6,128]{1,0:T(8,128)S(1)}, f32[6,128]{1,0:T(8,128)S(1)}, u32[]{:S(2)}, u32[]{:S(2)}) collective-permute-start(f32[6,128]{1,0:T(8,128)S(1)} %add_add_fusion.1), channel_id=1, source_target_pairs={{0,3},{1,0},{2,1},{3,2},{4,7},{5,4},{6,5},{7,6},{8,11},{9,8},{10,9... | collective-permute-start | bytes 9224 | tf_op jit(solution)/shard_map/ppermute | solution.py:27

commit v2 on v1

--- a/solution.py
+++ b/solution.py
@@ -83,6 +83,31 @@
         out_shape=jax.ShapeDtypeStruct((count, t + rows, LANES), jnp.bfloat16),
         name="pack_first",
     )(counts, in_acts, in_store)
+
+
+def cut_columns(map_order, value):
+    rows, full = value.shape
+    groups = 4
+    width, tile = full // groups, 128
+
+    def body(order_ref, *refs):
+        for g in range(groups):
+            refs[groups + g][...] = refs[g][...]
+
+    return pl.pallas_call(
+        body,
+        grid_spec=pltpu.PrefetchScalarGridSpec(
+            num_scalar_prefetch=1,
+            grid=(rows // tile,),
+            in_specs=[
+                pl.BlockSpec((tile, width), lambda i, o, g=g: (i, o[9 * g + 8]))
+                for g in range(groups)
+            ],
+            out_specs=[pl.BlockSpec((tile, width), lambda i, o: (i, 0))] * groups,
+        ),
+        out_shape=[jax.ShapeDtypeStruct((rows, width), value.dtype)] * groups,
+        name="cut_columns",
+    )(map_order, *[value] * groups)
 
 
 def pack_left(store, width):
@@ -310,11 +335,8 @@
     turn_order, map_order = orders(y, z, x, lax.axis_index("layer_1"))
 
     own = eigenvalues[0]
-    quarter = in_full // 4
-    got = []
-    for group in range(4):
-        part = lax.dynamic_slice_in_dim(own, map_order[9 * group + 8] * quarter, quarter, 1)
-        got.append(received(part))
+    parts = cut_columns(map_order, own)
+    got = [received(part) for part in parts]
 
     packed = pack_first(counts, in_acts[0], in_store[0].reshape(-1, in_full))
     first = lax.all_to_all(packed, DP, 0, 0, tiled=True)
@@ -346,7 +368,8 @@
     mapped = None
     for group, part in enumerate((both, b_before, b_after, b_far)):
         parts = (part, shifted(part, "layer_1", 1))
-        mapped = map_part(group, parts, map_order, (own, got[group]), left, mapped, left_rows)
+        eigens = (own, got[group])
+        mapped = map_part(group, parts, map_order, eigens, left, mapped, left_rows)
     totals = sum_everywhere(mapped.reshape(-1, LANES))
     return totals.reshape(NQ, WIN, R)
 

time: 239 us -> 242 us (1.013)
  Pallas kernels: 59.4 us -> 64.9 us
  local copies, waits for them, and re-layouts: 27.1 us -> 22.7 us
  between operations: 2.9 us -> 0.26 us
    pallas_call x0 -> x1, Pallas kernels: none -> 5.43 us  [cut_columns(): pl.pallas_call(body, grid_spec=pltpu.PrefetchScalarGridSpec(num_scalar_pr...]
    dynamic_slice x1 -> x0, local copies, waits for them, and re-layouts: 4.3 us -> none  [on_device(): lax.dynamic_slice_in_dim(own, map_order[9 * group + 8] * quarter, quarter...]
    unnamed x26 -> x28, local copies, waits for them, and re-layouts: 6.54 us -> 8.11 us
  transfers between devices with their start and end apart: 38 -> 38, of which waited for: 13 -> 13; matrix products, arithmetic and copies ran while one was open for 13% -> 11% of each run, Pallas kernels for 20% -> 22%
where the time goes in v2:
time: 242 us; the launch traced here: 240 us
  waiting for transfers between devices  73.5 us (30%)
  starting transfers between devices  70.6 us (29%)
  Pallas kernels  64.9 us (27%)
  local copies, waits for them, and re-layouts  22.7 us (9%)
  other arithmetic  8.22 us (3%)
    ppermute x29, waiting for transfers between devices, shifted(): lax.ppermute(value, axis, [(i, (i + step) % count) for i in range(count)])  73.5 us
    ppermute x29, starting transfers between devices, shifted(): lax.ppermute(value, axis, [(i, (i + step) % count) for i in range(count)])  44.3 us
    pallas_call x4, Pallas kernels, map_part(): pl.pallas_call(body, grid_spec=pltpu.PrefetchScalarGridSpec(num_scalar_pr...  28.6 us
    pallas_call x4, Pallas kernels, turn_part(): pl.pallas_call(body, grid_spec=pltpu.PrefetchScalarGridSpec(num_scalar_pr...  17.7 us
    ppermute x7, starting transfers between devices, received(): return lax.ppermute(value, ('layer_1', Z), [(1, 2), (2, 1)])  9.44 us
    all_to_all x1, starting transfers between devices, on_device(): first = lax.all_to_all(packed, DP, 0, 0, tiled=True)  9.03 us
    unnamed x28, local copies, waits for them, and re-layouts  8.11 us
    all_to_all x1, starting transfers between devices, on_device(): slices = lax.all_to_all(store, DP, 0, 0, tiled=True)  7.79 us
  transfers between devices with their start and end apart: 38, of which 13 were waited for; matrix products, arithmetic and copies ran while one was open for 11% of the time, Pallas kernels for 22%

profile of v2, /device:TPU:8, one launch (start us, length us, event | category | flops | bytes accessed | tf_op | source)
XLA Modules:
  0.0 240.2 jit_solution(12036977690198208678)
XLA Ops:
  0.0 4.1 %pack_first.1 = bf16[32,192,128]{2,1,0:T(8,128)(2,1)} custom-call(s32[2]{0:T(128)} %counts_ref.1, bf16[128,128]{1,0:T(8,128)(2,1)} %bitcast.57, bf16[64,4096]{1,0:T(8,128)(2,1)} %bitcast.51), custom_call_target="tpu_custom_call" | custom-call | tf_op jit(solution)/shard_map/pack_first/pallas_call | solution.py:72
  4.1 9.0 %all-to-all-start = ((bf16[32,192,128]{2,1,0:T(8,128)(2,1)}), bf16[32,192,128]{2,1,0:T(8,128)(2,1)S(1)}, u32[]{:S(2)}, u32[]{:S(2)}) async-start(bf16[32,192,128]{2,1,0:T(8,128)(2,1)} %pack_first.1), calls=%async_computation | async-start | bytes 3145728 | tf_op jit(solution)/shard_map/all_to_all | solution.py:342
  13.2 1.5 collective-permute-start.10
  14.8 19.7 %collective-permute-done.10 = bf16[128,512]{1,0:T(8,128)(2,1)S(1)} collective-permute-done((bf16[128,512]{1,0:T(8,128)(2,1)S(1)}, bf16[128,512]{1,0:T(8,128)(2,1)S(1)}, u32[]{:S(2)}, u32[]{:S(2)}) %collective-permute-start.10) | collective-permute-done | bytes 131104 | tf_op jit(solution)/shard_map/ppermute | solution.py:27
  34.5 1.5 collective-permute-start.11
  38.1 5.6 %pack_left.1 = bf16[32,64,512]{2,1,0:T(8,128)(2,1)} custom-call(bf16[64,16384]{1,0:T(8,128)(2,1)} %bitcast.48), custom_call_target="tpu_custom_call" | custom-call | tf_op jit(solution)/shard_map/pack_left/pallas_call | solution.py:122
  44.4 1.5 collective-permute-start.13
  46.6 1.2 copy-done
  47.8 7.8 %all-to-all-start.1 = ((bf16[32,64,512]{2,1,0:T(8,128)(2,1)}), bf16[32,64,512]{2,1,0:T(8,128)(2,1)}, u32[]{:S(2)}, u32[]{:S(2)}) async-start(bf16[32,64,512]{2,1,0:T(8,128)(2,1)} %pack_left.1), calls=%async_computation.1 | async-start | bytes 4194304 | tf_op jit(solution)/shard_map/all_to_all | solution.py:364
  55.6 0.7 constant_dynamic-update-slice_fusion.5
  57.0 3.6 %head.1 = bf16[896,128]{1,0:T(8,128)(2,1)} custom-call(s32[24]{0:T(128)} %reshape.118.winners_ref, bf16[32,192,128]{2,1,0:T(8,128)(2,1)} %copy-done, bf16[4096,128]{1,0:T(8,128)(2,1)} %bitcast.49), custom_call_target="tpu_custom_call" | custom-call | tf_op jit(solution)/shard_map/head/pallas_call | solution.py:151
  62.6 1.5 collective-permute-start.15
  64.0 1.8 collective-permute-start.17
  65.8 1.0 broadcast_select_fusion.1
  67.9 5.4 %cut_columns.1 = (bf16[512,1024]{1,0:T(8,128)(2,1)}, bf16[512,1024]{1,0:T(8,128)(2,1)}, bf16[512,1024]{1,0:T(8,128)(2,1)}, bf16[512,1024]{1,0:T(8,128)(2,1)}) custom-call(s32[37]{0:T(128)} %pad_add_fusion.1.order_ref, bf16[512,4096]{1,0:T(8,128)(2,1)} %bitcast.39, bf16[512,4096]{1,0:T(8,128)(2,1)} %bitcast.40, bf16[512,4096]{1,0:T(8,128)(2,1)} %bitcast.41, ...), custom_call_target="tpu_custom_call" | custom-call | tf_op jit(solution)/shard_map/cut_columns/pallas_call | solution.py:97
  73.3 1.6 collective-permute-start.25
  75.0 3.0 %collective-permute-start.2 = (bf16[896,128]{1,0:T(8,128)(2,1)S(1)}, bf16[896,128]{1,0:T(8,128)(2,1)S(1)}, u32[]{:S(2)}, u32[]{:S(2)}) collective-permute-start(bf16[896,128]{1,0:T(8,128)(2,1)S(1)} %broadcast_select_fusion.1), channel_id=1, source_target_pairs={{0,3},{1,0},{2,1},{3,2},{4,7},{5,4},{6,5},{7,6},{8,11},{9,8},{10,9... | collective-permute-start | bytes 688136 | tf_op jit(solution)/shard_map/ppermute | solution.py:27
  78.0 29.0 %collective-permute-done.1 = bf16[896,128]{1,0:T(8,128)(2,1)S(1)} collective-permute-done((bf16[896,128]{1,0:T(8,128)(2,1)S(1)}, bf16[896,128]{1,0:T(8,128)(2,1)S(1)}, u32[]{:S(2)}, u32[]{:S(2)}) %collective-permute-start.1) | collective-permute-done | bytes 229408 | tf_op jit(solution)/shard_map/ppermute | solution.py:27
  107.0 0.9 collective-permute-start.3
  107.9 6.6 %collective-permute-done.3 = bf16[896,128]{1,0:T(8,128)(2,1)S(1)} collective-permute-done((bf16[896,128]{1,0:T(8,128)(2,1)S(1)}, bf16[896,128]{1,0:T(8,128)(2,1)S(1)}, u32[]{:S(2)}, u32[]{:S(2)}) %collective-permute-start.3) | collective-permute-done | bytes 229408 | tf_op jit(solution)/shard_map/ppermute | solution.py:27
  115.2 1.2 pad_maximum_fusion.1.near_ref
  116.4 1.5 collective-permute-start.4
  118.5 0.9 slice.30
  119.6 1.7 collective-permute-start.23
  121.4 2.2 gather_fusion
  124.2 3.3 %collective-permute-start.18 = (bf16[4,128,512]{2,1,0:T(8,128)(2,1)S(1)}, bf16[4,128,512]{2,1,0:T(8,128)(2,1)}, u32[]{:S(2)}, u32[]{:S(2)}) collective-permute-start(bf16[4,128,512]{2,1,0:T(8,128)(2,1)S(1)} %slice.31), channel_id=1, source_target_pairs={{0,3},{1,0},{2,1},{3,2},{4,7},{5,4},{6,5},{7,6},{8,11},{9,8},{10,9... | collective-permute-start | bytes 1572872 | tf_op jit(solution)/shard_map/ppermute | solution.py:27
  127.6 1.2 copy.18
  128.8 2.6 %collective-permute-done.16 = bf16[4,128,512]{2,1,0:T(8,128)(2,1)} collective-permute-done((bf16[4,128,512]{2,1,0:T(8,128)(2,1)}, bf16[4,128,512]{2,1,0:T(8,128)(2,1)}, u32[]{:S(2)}, u32[]{:S(2)}) %collective-permute-start.16) | collective-permute-done | bytes 524320 | tf_op jit(solution)/shard_map/ppermute | solution.py:27
  131.5 4.6 %collective-permute-done.4.near_ref = bf16[4,896,128]{2,1,0:T(8,128)(2,1)} collective-permute-done((bf16[4,896,128]{2,1,0:T(8,128)(2,1)S(1)}, bf16[4,896,128]{2,1,0:T(8,128)(2,1)}, u32[]{:S(2)}, u32[]{:S(2)}) %collective-permute-start.4) | collective-permute-done | bytes 917536 | tf_op jit(solution)/shard_map/ppermute | solution.py:27
  136.1 1.5 collective-permute-start.26
  138.3 1.8 slice.26
  140.1 1.5 collective-permute-start.5
  141.6 4.3 %turn_part.4.refs_4_ = f32[128,512]{1,0:T(8,128)} custom-call(s32[32]{0:T(128)} %add.164.order_ref, bf16[8,128,512]{2,1,0:T(8,128)(2,1)} %constant_dynamic-update-slice_fusion.2.value_ref, bf16[16384,512]{1,0:T(8,128)(2,1)} %bitcast.23, bf16[16384,512]{1,0:T(8,128)(2,1)} %bitcast.24, bf16[16384,512]{1,0:T(8,128)(2,1)} %bitcast.25, bf16[16384,512]{1,0:T(8,128)(2,1)} %bitcast.26), custom_call_target="tpu_custom_call" | custom-call | flops 536870912 | bytes 4194304 | tf_op jit(solution)/shard_map/turn_part/pallas_call | solution.py:193
  145.9 4.5 %turn_part.5.refs_4_ = f32[128,512]{1,0:T(8,128)} custom-call(s32[32]{0:T(128)} %add.164.order_ref, bf16[8,128,512]{2,1,0:T(8,128)(2,1)} %copy-done.3, bf16[16384,512]{1,0:T(8,128)(2,1)} %bitcast.27, bf16[16384,512]{1,0:T(8,128)(2,1)} %bitcast.28, bf16[16384,512]{1,0:T(8,128)(2,1)} %bitcast.29, bf16[16384,512]{1,0:T(8,128)(2,1)} %bitcast.30, ...), custom_call_target="tpu_custom_call" | custom-call | flops 536870912 | bytes 4194304 | tf_op jit(solution)/shard_map/turn_part/pallas_call | solution.py:193
  150.4 1.8 slice.27
  152.8 4.5 %turn_part.6.refs_4_ = f32[128,512]{1,0:T(8,128)} custom-call(s32[32]{0:T(128)} %add.164.order_ref, bf16[8,128,512]{2,1,0:T(8,128)(2,1)} %copy-done.2, bf16[16384,512]{1,0:T(8,128)(2,1)} %bitcast.31, bf16[16384,512]{1,0:T(8,128)(2,1)} %bitcast.32, bf16[16384,512]{1,0:T(8,128)(2,1)} %bitcast.33, bf16[16384,512]{1,0:T(8,128)(2,1)} %bitcast.34, ...), custom_call_target="tpu_custom_call" | custom-call | flops 536870912 | bytes 4194304 | tf_op jit(solution)/shard_map/turn_part/pallas_call | solution.py:193
  157.2 2.3 pad_maximum_fusion.value_ref
  159.5 4.4 %turn_part.7 = bf16[128,512]{1,0:T(8,128)(2,1)} custom-call(s32[32]{0:T(128)} %add.164.order_ref, bf16[8,128,512]{2,1,0:T(8,128)(2,1)} %pad_maximum_fusion.value_ref, bf16[16384,512]{1,0:T(8,128)(2,1)} %bitcast.35, bf16[16384,512]{1,0:T(8,128)(2,1)} %bitcast.36, bf16[16384,512]{1,0:T(8,128)(2,1)} %bitcast.37, bf16[16384,512]{1,0:T(8,128)(2,1)} %bitcast.38, ...), custom_call_target="tpu_custom_call" | custom-call | flops 536870912 | bytes 4194304 | tf_op jit(solution)/shard_map/turn_part/pallas_call | solution.py:193
  164.6 1.6 collective-permute-start.21
  166.2 8.2 %collective-permute-start.22 = (bf16[4,896,128]{2,1,0:T(8,128)(2,1)}, bf16[4,896,128]{2,1,0:T(8,128)(2,1)}, u32[]{:S(2)}, u32[]{:S(2)}) collective-permute-start(bf16[4,896,128]{2,1,0:T(8,128)(2,1)} %collective-permute-done.4.near_ref), channel_id=1, source_target_pairs={{0,32},{32,0},{1,33},{33,1},{2,34},{34,2},{3,35},{35,3},{4,36},{36... | collective-permute-start | bytes 2752520 | tf_op jit(solution)/shard_map/ppermute | solution.py:27
  174.4 1.8 constant_dynamic-update-slice_fusion.1
  176.2 0.8 constant_dynamic-update-slice_fusion.near_ref
  177.1 1.6 collective-permute-start.9
  178.7 2.1 collective-permute-start.8
  180.8 1.6 broadcast_select_fusion.2.left_ref
  182.4 1.4 copy.19
  183.8 1.1 broadcast_select_fusion.refs_1_
  184.9 6.5 %map_part.4.refs_0_ = f32[4,512,192]{2,1,0:T(8,128)} custom-call(s32[37]{0:T(128)} %pad_add_fusion.1.order_ref, bf16[4,896,128]{2,1,0:T(8,128)(2,1)} %copy-done.1, bf16[4,896,128]{2,1,0:T(8,128)(2,1)} %copy-done.4, bf16[512,4096]{1,0:T(8,128)(2,1)} %bitcast.43, bf16[512,1024]{1,0:T(8,128)(2,1)} %collective-permute-done.25.got_ref, ...), custom_call_target="tpu_custom_call" | custom-call | flops 1879048192 | bytes 1048576 | tf_op jit(solution)/shard_map/map_part/pallas_call | solution.py:297
  191.4 6.8 %map_part.5.refs_0_ = f32[4,512,192]{2,1,0:T(8,128)} custom-call(s32[37]{0:T(128)} %pad_add_fusion.1.order_ref, bf16[4,896,128]{2,1,0:T(8,128)(2,1)} %collective-permute-done.4.near_ref, bf16[4,896,128]{2,1,0:T(8,128)(2,1)} %collective-permute-done.22.far_ref, bf16[512,4096]{1,0:T(8,128)(2,1)} %bitcast.44, ...), custom_call_target="tpu_custom_call" | custom-call | flops 1879048192 | bytes 1048576 | tf_op jit(solution)/shard_map/map_part/pallas_call | solution.py:297
  198.2 6.9 %map_part.6.refs_0_ = f32[4,512,192]{2,1,0:T(8,128)} custom-call(s32[37]{0:T(128)} %pad_add_fusion.1.order_ref, bf16[4,896,128]{2,1,0:T(8,128)(2,1)} %collective-permute-done.6.near_ref, bf16[4,896,128]{2,1,0:T(8,128)(2,1)} %collective-permute-done.20.far_ref, bf16[512,4096]{1,0:T(8,128)(2,1)} %bitcast.45, ...), custom_call_target="tpu_custom_call" | custom-call | flops 1879048192 | bytes 1048576 | tf_op jit(solution)/shard_map/map_part/pallas_call | solution.py:297
  205.1 0.9 copy-done.5
  206.0 8.4 %map_part.7 = f32[4,192]{1,0:T(4,128)} custom-call(s32[37]{0:T(128)} %pad_add_fusion.1.order_ref, bf16[4,896,128]{2,1,0:T(8,128)(2,1)} %constant_dynamic-update-slice_fusion.near_ref, bf16[4,896,128]{2,1,0:T(8,128)(2,1)} %copy-done.5, bf16[512,4096]{1,0:T(8,128)(2,1)} %bitcast.46, bf16[512,1024]{1,0:T(8,128)(2,1)} %collective-permute-done.9.got_ref, ...), custom_call_target="tpu_custom_call" | custom-call | flops 1879048192 | bytes 1048576 | tf_op jit(solution)/shard_map/map_part/pallas_call | solution.py:297
  214.4 0.8 reshape.121
  215.3 1.1 collective-permute-done.27
  216.9 3.1 %collective-permute-done.28 = f32[6,128]{1,0:T(8,128)S(1)} collective-permute-done((f32[6,128]{1,0:T(8,128)S(1)}, f32[6,128]{1,0:T(8,128)S(1)}, u32[]{:S(2)}, u32[]{:S(2)}) %collective-permute-start.28) | collective-permute-done | bytes 3104 | tf_op jit(solution)/shard_map/ppermute | solution.py:27
  219.9 3.6 %collective-permute-start.29 = (f32[6,128]{1,0:T(8,128)S(1)}, f32[6,128]{1,0:T(8,128)S(1)}, u32[]{:S(2)}, u32[]{:S(2)}) collective-permute-start(f32[6,128]{1,0:T(8,128)S(1)} %add.168), channel_id=1, source_target_pairs={{0,64},{64,0},{1,65},{65,1},{2,66},{66,2},{3,67},{67,3},{4,68},{68... | collective-permute-start | bytes 9224 | tf_op jit(solution)/shard_map/ppermute | solution.py:27
  223.5 1.6 collective-permute-done.29
  225.1 2.0 collective-permute-start.30
  227.2 2.3 collective-permute-start.31
  229.5 0.8 collective-permute-done.30
  230.8 2.3 collective-permute-done.32
  233.1 1.6 collective-permute-start.33
  234.7 3.2 %collective-permute-start.35 = (f32[6,128]{1,0:T(8,128)S(1)}, f32[6,128]{1,0:T(8,128)S(1)}, u32[]{:S(2)}, u32[]{:S(2)}) collective-permute-start(f32[6,128]{1,0:T(8,128)S(1)} %add_add_fusion.1), channel_id=1, source_target_pairs={{0,3},{1,0},{2,1},{3,2},{4,7},{5,4},{6,5},{7,6},{8,11},{9,8},{10,9... | collective-permute-start | bytes 9224 | tf_op jit(solution)/shard_map/ppermute | solution.py:27
  238.2 1.3 collective-permute-done.34
  (99 shorter events, 13.7 us)
Async XLA Ops:
  4.1 9.1 %copy-start.6 = (bf16[1,128,512]{2,1,0:T(8,128)(2,1)S(1)}, bf16[1,128,512]{2,1,0:T(8,128)(2,1)}, u32[]{:S(2)}) copy-start(bf16[1,128,512]{2,1,0:T(8,128)(2,1)} %param.11) | copy-start | bytes 393220
  4.1 10.6 %copy-start.10 = (s32[4]{0:T(128)S(1)}, s32[4]{0:T(128)}, u32[]{:S(2)}) copy-start(s32[4]{0:T(128)} %constant.80.clone) | copy-start | bytes 52
  4.1 33.2 %copy-start.9 = (s32[4,6]{1,0:T(4,128)S(1)}, s32[4,6]{1,0:T(4,128)}, u32[]{:S(2)}) copy-start(s32[4,6]{1,0:T(4,128)} %param.19) | copy-start | bytes 292
  4.1 42.4 %all-to-all-start = ((bf16[32,192,128]{2,1,0:T(8,128)(2,1)}), bf16[32,192,128]{2,1,0:T(8,128)(2,1)S(1)}, u32[]{:S(2)}, u32[]{:S(2)}) async-start(bf16[32,192,128]{2,1,0:T(8,128)(2,1)} %pack_first.1), calls=%async_computation | async-start | bytes 3145728 | tf_op jit(solution)/shard_map/all_to_all | solution.py:342
  13.2 21.3 %collective-permute-start.10 = (bf16[128,512]{1,0:T(8,128)(2,1)S(1)}, bf16[128,512]{1,0:T(8,128)(2,1)S(1)}, u32[]{:S(2)}, u32[]{:S(2)}) collective-permute-start(bf16[128,512]{1,0:T(8,128)(2,1)S(1)} %bitcast.52), channel_id=1, source_target_pairs={{0,4},{4,0},{1,5},{5,1},{2,6},{6,2},{3,7},{7,3},{8,12},{12,8},{9,1... | collective-permute-start | bytes 393224 | tf_op jit(solution)/shard_map/ppermute | solution.py:27
  34.5 9.8 %collective-permute-start.11 = (bf16[2,128,512]{2,1,0:T(8,128)(2,1)S(1)}, bf16[2,128,512]{2,1,0:T(8,128)(2,1)S(1)}, u32[]{:S(2)}, u32[]{:S(2)}) collective-permute-start(bf16[2,128,512]{2,1,0:T(8,128)(2,1)S(1)} %pad_maximum_fusion.2), channel_id=1, source_target_pairs={{0,8},{8,16},{16,24},{24,0},{1,9},{9,17},{17,25},{25,1},{2,10},{10... | collective-permute-start | bytes 786440 | tf_op jit(solution)/shard_map/ppermute | solution.py:27
  36.1 9.8 %collective-permute-start.12 = (bf16[2,128,512]{2,1,0:T(8,128)(2,1)S(1)}, bf16[2,128,512]{2,1,0:T(8,128)(2,1)S(1)}, u32[]{:S(2)}, u32[]{:S(2)}) collective-permute-start(bf16[2,128,512]{2,1,0:T(8,128)(2,1)S(1)} %pad_maximum_fusion.2), channel_id=1, source_target_pairs={{0,24},{8,0},{16,8},{24,16},{1,25},{9,1},{17,9},{25,17},{2,26},{10... | collective-permute-start | bytes 786440 | tf_op jit(solution)/shard_map/ppermute | solution.py:27
  44.4 16.8 %collective-permute-start.13 = (bf16[1,128,512]{2,1,0:T(8,128)(2,1)S(1)}, bf16[1,128,512]{2,1,0:T(8,128)(2,1)S(1)}, u32[]{:S(2)}, u32[]{:S(2)}) collective-permute-start(bf16[1,128,512]{2,1,0:T(8,128)(2,1)S(1)} %slice.28), channel_id=1, source_target_pairs={{0,8},{8,16},{16,24},{24,0},{1,9},{9,17},{17,25},{25,1},{2,10},{10... | collective-permute-start | bytes 393224 | tf_op jit(solution)/shard_map/ppermute | solution.py:27
  45.9 16.0 %collective-permute-start.14 = (bf16[1,128,512]{2,1,0:T(8,128)(2,1)S(1)}, bf16[1,128,512]{2,1,0:T(8,128)(2,1)S(1)}, u32[]{:S(2)}, u32[]{:S(2)}) collective-permute-start(bf16[1,128,512]{2,1,0:T(8,128)(2,1)S(1)} %slice.29), channel_id=1, source_target_pairs={{0,24},{8,0},{16,8},{24,16},{1,25},{9,1},{17,9},{25,17},{2,26},{10... | collective-permute-start | bytes 393224 | tf_op jit(solution)/shard_map/ppermute | solution.py:27
  46.6 1.2 copy-start
  47.8 73.6 %all-to-all-start.1 = ((bf16[32,64,512]{2,1,0:T(8,128)(2,1)}), bf16[32,64,512]{2,1,0:T(8,128)(2,1)}, u32[]{:S(2)}, u32[]{:S(2)}) async-start(bf16[32,64,512]{2,1,0:T(8,128)(2,1)} %pack_left.1), calls=%async_computation.1 | async-start | bytes 4194304 | tf_op jit(solution)/shard_map/all_to_all | solution.py:364
  60.6 5.2 %collective-permute-start = (bf16[896,128]{1,0:T(8,128)(2,1)}, bf16[896,128]{1,0:T(8,128)(2,1)S(1)}, u32[]{:S(2)}, u32[]{:S(2)}) collective-permute-start(bf16[896,128]{1,0:T(8,128)(2,1)} %head.1), channel_id=1, source_target_pairs={{4,32},{32,4},{5,33},{33,5},{6,34},{34,6},{7,35},{35,7},{12,40},{4... | collective-permute-start | bytes 688136 | tf_op jit(solution)/shard_map/ppermute | solution.py:49
  62.6 55.9 %collective-permute-start.15 = (bf16[8,128,512]{2,1,0:T(8,128)(2,1)}, bf16[8,128,512]{2,1,0:T(8,128)(2,1)S(1)}, u32[]{:S(2)}, u32[]{:S(2)}) collective-permute-start(bf16[8,128,512]{2,1,0:T(8,128)(2,1)} %constant_dynamic-update-slice_fusion.2.value_ref), channel_id=1, source_target_pairs={{0,1},{1,2},{2,3},{3,0},{4,5},{5,6},{6,7},{7,4},{8,9},{9,10},{10,1... | collective-permute-start | bytes 3145736 | tf_op jit(solution)/shard_map/ppermute | solution.py:27
  64.0 55.6 %collective-permute-start.17 = (bf16[8,128,512]{2,1,0:T(8,128)(2,1)}, bf16[8,128,512]{2,1,0:T(8,128)(2,1)S(1)}, u32[]{:S(2)}, u32[]{:S(2)}) collective-permute-start(bf16[8,128,512]{2,1,0:T(8,128)(2,1)} %constant_dynamic-update-slice_fusion.2.value_ref), channel_id=1, source_target_pairs={{0,3},{1,0},{2,1},{3,2},{4,7},{5,4},{6,5},{7,6},{8,11},{9,8},{10,9... | collective-permute-start | bytes 3145736 | tf_op jit(solution)/shard_map/ppermute | solution.py:27
  66.8 40.2 %collective-permute-start.1 = (bf16[896,128]{1,0:T(8,128)(2,1)S(1)}, bf16[896,128]{1,0:T(8,128)(2,1)S(1)}, u32[]{:S(2)}, u32[]{:S(2)}) collective-permute-start(bf16[896,128]{1,0:T(8,128)(2,1)S(1)} %broadcast_select_fusion.1), channel_id=1, source_target_pairs={{0,1},{1,2},{2,3},{3,0},{4,5},{5,6},{6,7},{7,4},{8,9},{9,10},{10,1... | collective-permute-start | bytes 688136 | tf_op jit(solution)/shard_map/ppermute | solution.py:27
  73.3 50.8 %collective-permute-start.25 = (bf16[512,1024]{1,0:T(8,128)(2,1)}, bf16[512,1024]{1,0:T(8,128)(2,1)}, u32[]{:S(2)}, u32[]{:S(2)}) collective-permute-start(bf16[512,1024]{1,0:T(8,128)(2,1)} %get-tuple-element.12), channel_id=1, source_target_pairs={{4,32},{32,4},{5,33},{33,5},{6,34},{34,6},{7,35},{35,7},{12,40},{4... | collective-permute-start | bytes 3145736 | tf_op jit(solution)/shard_map/ppermute | solution.py:49
  75.0 32.9 %collective-permute-start.2 = (bf16[896,128]{1,0:T(8,128)(2,1)S(1)}, bf16[896,128]{1,0:T(8,128)(2,1)S(1)}, u32[]{:S(2)}, u32[]{:S(2)}) collective-permute-start(bf16[896,128]{1,0:T(8,128)(2,1)S(1)} %broadcast_select_fusion.1), channel_id=1, source_target_pairs={{0,3},{1,0},{2,1},{3,2},{4,7},{5,4},{6,5},{7,6},{8,11},{9,8},{10,9... | collective-permute-start | bytes 688136 | tf_op jit(solution)/shard_map/ppermute | solution.py:27
  107.0 7.5 %collective-permute-start.3 = (bf16[896,128]{1,0:T(8,128)(2,1)S(1)}, bf16[896,128]{1,0:T(8,128)(2,1)S(1)}, u32[]{:S(2)}, u32[]{:S(2)}) collective-permute-start(bf16[896,128]{1,0:T(8,128)(2,1)S(1)} %broadcast_select_fusion.1), channel_id=1, source_target_pairs={{0,2},{1,3},{2,0},{3,1},{4,6},{5,7},{6,4},{7,5},{8,10},{9,11},{10,... | collective-permute-start | bytes 688136 | tf_op jit(solution)/shard_map/ppermute | solution.py:27
  107.9 6.6 %copy-start.7 = (bf16[896,128]{1,0:T(8,128)(2,1)}, bf16[896,128]{1,0:T(8,128)(2,1)S(1)}, u32[]{:S(2)}) copy-start(bf16[896,128]{1,0:T(8,128)(2,1)S(1)} %collective-permute-done.2) | copy-start | bytes 688132
  114.5 0.7 copy-start.8
  116.4 15.1 %copy-start.1 = (bf16[4,896,128]{2,1,0:T(8,128)(2,1)}, bf16[4,896,128]{2,1,0:T(8,128)(2,1)S(1)}, u32[]{:S(2)}) copy-start(bf16[4,896,128]{2,1,0:T(8,128)(2,1)S(1)} %pad_maximum_fusion.1.near_ref) | copy-start | bytes 2752516
  116.4 19.7 %collective-permute-start.4 = (bf16[4,896,128]{2,1,0:T(8,128)(2,1)S(1)}, bf16[4,896,128]{2,1,0:T(8,128)(2,1)}, u32[]{:S(2)}, u32[]{:S(2)}) collective-permute-start(bf16[4,896,128]{2,1,0:T(8,128)(2,1)S(1)} %pad_maximum_fusion.1.near_ref), channel_id=1, source_target_pairs={{0,8},{8,16},{16,24},{24,0},{1,9},{9,17},{17,25},{25,1},{2,10},{10... | collective-permute-start | bytes 2752520 | tf_op jit(solution)/shard_map/ppermute | solution.py:27
  117.9 22.2 %collective-permute-start.6 = (bf16[4,896,128]{2,1,0:T(8,128)(2,1)S(1)}, bf16[4,896,128]{2,1,0:T(8,128)(2,1)}, u32[]{:S(2)}, u32[]{:S(2)}) collective-permute-start(bf16[4,896,128]{2,1,0:T(8,128)(2,1)S(1)} %pad_maximum_fusion.1.near_ref), channel_id=1, source_target_pairs={{0,24},{8,0},{16,8},{24,16},{1,25},{9,1},{17,9},{25,17},{2,26},{10... | collective-permute-start | bytes 2752520 | tf_op jit(solution)/shard_map/ppermute | solution.py:27
  118.5 2.9 %copy-start.3 = (bf16[8,128,512]{2,1,0:T(8,128)(2,1)}, bf16[8,128,512]{2,1,0:T(8,128)(2,1)S(1)}, u32[]{:S(2)}) copy-start(bf16[8,128,512]{2,1,0:T(8,128)(2,1)S(1)} %collective-permute-done.15.value_ref) | copy-start | bytes 3145732
  119.4 12.1 %collective-permute-start.16 = (bf16[4,128,512]{2,1,0:T(8,128)(2,1)}, bf16[4,128,512]{2,1,0:T(8,128)(2,1)}, u32[]{:S(2)}, u32[]{:S(2)}) collective-permute-start(bf16[4,128,512]{2,1,0:T(8,128)(2,1)} %slice.30), channel_id=1, source_target_pairs={{0,1},{1,2},{2,3},{3,0},{4,5},{5,6},{6,7},{7,4},{8,9},{9,10},{10,1... | collective-permute-start | bytes 1572872 | tf_op jit(solution)/shard_map/ppermute | solution.py:27
  119.6 4.0 %copy-start.2 = (bf16[8,128,512]{2,1,0:T(8,128)(2,1)}, bf16[8,128,512]{2,1,0:T(8,128)(2,1)S(1)}, u32[]{:S(2)}) copy-start(bf16[8,128,512]{2,1,0:T(8,128)(2,1)S(1)} %collective-permute-done.17.value_ref) | copy-start | bytes 3145732
  119.6 44.3 %collective-permute-start.23 = (bf16[512,1024]{1,0:T(8,128)(2,1)}, bf16[512,1024]{1,0:T(8,128)(2,1)}, u32[]{:S(2)}, u32[]{:S(2)}) collective-permute-start(bf16[512,1024]{1,0:T(8,128)(2,1)} %get-tuple-element.11), channel_id=1, source_target_pairs={{4,32},{32,4},{5,33},{33,5},{6,34},{34,6},{7,35},{35,7},{12,40},{4... | collective-permute-start | bytes 3145736 | tf_op jit(solution)/shard_map/ppermute | solution.py:49
  124.2 28.1 %collective-permute-start.18 = (bf16[4,128,512]{2,1,0:T(8,128)(2,1)S(1)}, bf16[4,128,512]{2,1,0:T(8,128)(2,1)}, u32[]{:S(2)}, u32[]{:S(2)}) collective-permute-start(bf16[4,128,512]{2,1,0:T(8,128)(2,1)S(1)} %slice.31), channel_id=1, source_target_pairs={{0,3},{1,0},{2,1},{3,2},{4,7},{5,4},{6,5},{7,6},{8,11},{9,8},{10,9... | collective-permute-start | bytes 1572872 | tf_op jit(solution)/shard_map/ppermute | solution.py:27
  131.5 47.2 %collective-permute-start.24 = (bf16[4,896,128]{2,1,0:T(8,128)(2,1)S(1)}, bf16[4,896,128]{2,1,0:T(8,128)(2,1)S(1)}, u32[]{:S(2)}, u32[]{:S(2)}) collective-permute-start(bf16[4,896,128]{2,1,0:T(8,128)(2,1)S(1)} %pad_maximum_fusion.1.near_ref), channel_id=1, source_target_pairs={{0,32},{32,0},{1,33},{33,1},{2,34},{34,2},{3,35},{35,3},{4,36},{36... | collective-permute-start | bytes 2752520 | tf_op jit(solution)/shard_map/ppermute | solution.py:27
  136.1 41.0 %collective-permute-start.26 = (bf16[4,512,192]{1,2,0:T(8,128)(2,1)}, bf16[4,512,192]{1,2,0:T(8,128)(2,1)}, u32[]{:S(2)}, u32[]{:S(2)}) collective-permute-start(bf16[4,512,192]{1,2,0:T(8,128)(2,1)} %copy.18), channel_id=1, source_target_pairs={{4,32},{32,4},{5,33},{33,5},{6,34},{34,6},{7,35},{35,7},{12,40},{4... | collective-permute-start | bytes 2359304 | tf_op jit(solution)/shard_map/ppermute | solution.py:49
  140.1 26.1 %collective-permute-start.5 = (bf16[2,896,128]{2,1,0:T(8,128)(2,1)}, bf16[2,896,128]{2,1,0:T(8,128)(2,1)}, u32[]{:S(2)}, u32[]{:S(2)}) collective-permute-start(bf16[2,896,128]{2,1,0:T(8,128)(2,1)} %slice.26), channel_id=1, source_target_pairs={{0,8},{8,16},{16,24},{24,0},{1,9},{9,17},{17,25},{25,1},{2,10},{10... | collective-permute-start | bytes 1376264 | tf_op jit(solution)/shard_map/ppermute | solution.py:27
  152.2 24.0 %collective-permute-start.7 = (bf16[2,896,128]{2,1,0:T(8,128)(2,1)}, bf16[2,896,128]{2,1,0:T(8,128)(2,1)S(1)}, u32[]{:S(2)}, u32[]{:S(2)}) collective-permute-start(bf16[2,896,128]{2,1,0:T(8,128)(2,1)} %slice.27), channel_id=1, source_target_pairs={{0,24},{8,0},{16,8},{24,16},{1,25},{9,1},{17,9},{25,17},{2,26},{10... | collective-permute-start | bytes 1376264 | tf_op jit(solution)/shard_map/ppermute | solution.py:27
  163.9 0.7 collective-permute-start.19
  164.6 33.6 %collective-permute-start.21 = (bf16[512,1024]{1,0:T(8,128)(2,1)}, bf16[512,1024]{1,0:T(8,128)(2,1)}, u32[]{:S(2)}, u32[]{:S(2)}) collective-permute-start(bf16[512,1024]{1,0:T(8,128)(2,1)} %get-tuple-element.10), channel_id=1, source_target_pairs={{4,32},{32,4},{5,33},{33,5},{6,34},{34,6},{7,35},{35,7},{12,40},{4... | collective-permute-start | bytes 3145736 | tf_op jit(solution)/shard_map/ppermute | solution.py:49
  166.2 25.2 %collective-permute-start.22 = (bf16[4,896,128]{2,1,0:T(8,128)(2,1)}, bf16[4,896,128]{2,1,0:T(8,128)(2,1)}, u32[]{:S(2)}, u32[]{:S(2)}) collective-permute-start(bf16[4,896,128]{2,1,0:T(8,128)(2,1)} %collective-permute-done.4.near_ref), channel_id=1, source_target_pairs={{0,32},{32,0},{1,33},{33,1},{2,34},{34,2},{3,35},{35,3},{4,36},{36... | collective-permute-start | bytes 2752520 | tf_op jit(solution)/shard_map/ppermute | solution.py:27
  176.2 22.0 %collective-permute-start.20 = (bf16[4,896,128]{2,1,0:T(8,128)(2,1)}, bf16[4,896,128]{2,1,0:T(8,128)(2,1)}, u32[]{:S(2)}, u32[]{:S(2)}) collective-permute-start(bf16[4,896,128]{2,1,0:T(8,128)(2,1)} %collective-permute-done.6.near_ref), channel_id=1, source_target_pairs={{0,32},{32,0},{1,33},{33,1},{2,34},{34,2},{3,35},{35,3},{4,36},{36... | collective-permute-start | bytes 2752520 | tf_op jit(solution)/shard_map/ppermute | solution.py:27
  177.1 28.1 %collective-permute-start.9 = (bf16[512,1024]{1,0:T(8,128)(2,1)}, bf16[512,1024]{1,0:T(8,128)(2,1)}, u32[]{:S(2)}, u32[]{:S(2)}) collective-permute-start(bf16[512,1024]{1,0:T(8,128)(2,1)} %get-tuple-element.9), channel_id=1, source_target_pairs={{4,32},{32,4},{5,33},{33,5},{6,34},{34,6},{7,35},{35,7},{12,40},{4... | collective-permute-start | bytes 3145736 | tf_op jit(solution)/shard_map/ppermute | solution.py:49
  178.7 2.1 copy-start.4
  178.7 26.4 %collective-permute-start.8 = (bf16[4,896,128]{2,1,0:T(8,128)(2,1)}, bf16[4,896,128]{2,1,0:T(8,128)(2,1)S(1)}, u32[]{:S(2)}, u32[]{:S(2)}) collective-permute-start(bf16[4,896,128]{2,1,0:T(8,128)(2,1)} %constant_dynamic-update-slice_fusion.near_ref), channel_id=1, source_target_pairs={{0,32},{32,0},{1,33},{33,1},{2,34},{34,2},{3,35},{35,3},{4,36},{36... | collective-permute-start | bytes 2752520 | tf_op jit(solution)/shard_map/ppermute | solution.py:27
  205.1 0.9 copy-start.5
  215.2 1.2 collective-permute-start.27
  216.3 3.6 %collective-permute-start.28 = (f32[6,128]{1,0:T(8,128)S(1)}, f32[6,128]{1,0:T(8,128)S(1)}, u32[]{:S(2)}, u32[]{:S(2)}) collective-permute-start(f32[6,128]{1,0:T(8,128)S(1)} %add.167), channel_id=1, source_target_pairs={{0,4},{4,0},{1,5},{5,1},{2,6},{6,2},{3,7},{7,3},{8,12},{12,8},{9,1... | collective-permute-start | bytes 9224 | tf_op jit(solution)/shard_map/ppermute | solution.py:27
  219.9 5.2 %collective-permute-start.29 = (f32[6,128]{1,0:T(8,128)S(1)}, f32[6,128]{1,0:T(8,128)S(1)}, u32[]{:S(2)}, u32[]{:S(2)}) collective-permute-start(f32[6,128]{1,0:T(8,128)S(1)} %add.168), channel_id=1, source_target_pairs={{0,64},{64,0},{1,65},{65,1},{2,66},{66,2},{3,67},{67,3},{4,68},{68... | collective-permute-start | bytes 9224 | tf_op jit(solution)/shard_map/ppermute | solution.py:27
  225.1 5.1 %collective-permute-start.30 = (f32[6,128]{1,0:T(8,128)S(1)}, f32[6,128]{1,0:T(8,128)S(1)}, u32[]{:S(2)}, u32[]{:S(2)}) collective-permute-start(f32[6,128]{1,0:T(8,128)S(1)} %add.169), channel_id=1, source_target_pairs={{0,16},{8,24},{16,0},{24,8},{1,17},{9,25},{17,1},{25,9},{2,18},{10... | collective-permute-start | bytes 9224 | tf_op jit(solution)/shard_map/ppermute | solution.py:27
  227.2 3.6 %collective-permute-start.31 = (f32[6,128]{1,0:T(8,128)S(1)}, f32[6,128]{1,0:T(8,128)S(1)}, u32[]{:S(2)}, u32[]{:S(2)}) collective-permute-start(f32[6,128]{1,0:T(8,128)S(1)} %add.169), channel_id=1, source_target_pairs={{0,8},{8,16},{16,24},{24,0},{1,9},{9,17},{17,25},{25,1},{2,10},{10... | collective-permute-start | bytes 9224 | tf_op jit(solution)/shard_map/ppermute | solution.py:27
  229.5 3.6 %collective-permute-start.32 = (f32[6,128]{1,0:T(8,128)S(1)}, f32[6,128]{1,0:T(8,128)S(1)}, u32[]{:S(2)}, u32[]{:S(2)}) collective-permute-start(f32[6,128]{1,0:T(8,128)S(1)} %add.169), channel_id=1, source_target_pairs={{0,24},{8,0},{16,8},{24,16},{1,25},{9,1},{17,9},{25,17},{2,26},{10... | collective-permute-start | bytes 9224 | tf_op jit(solution)/shard_map/ppermute | solution.py:27
  233.1 5.1 %collective-permute-start.33 = (f32[6,128]{1,0:T(8,128)S(1)}, f32[6,128]{1,0:T(8,128)S(1)}, u32[]{:S(2)}, u32[]{:S(2)}) collective-permute-start(f32[6,128]{1,0:T(8,128)S(1)} %add_add_fusion.1), channel_id=1, source_target_pairs={{0,2},{1,3},{2,0},{3,1},{4,6},{5,7},{6,4},{7,5},{8,10},{9,11},{10,... | collective-permute-start | bytes 9224 | tf_op jit(solution)/shard_map/ppermute | solution.py:27
  234.7 4.8 %collective-permute-start.34 = (f32[6,128]{1,0:T(8,128)S(1)}, f32[6,128]{1,0:T(8,128)S(1)}, u32[]{:S(2)}, u32[]{:S(2)}) collective-permute-start(f32[6,128]{1,0:T(8,128)S(1)} %add_add_fusion.1), channel_id=1, source_target_pairs={{0,1},{1,2},{2,3},{3,0},{4,5},{5,6},{6,7},{7,4},{8,9},{9,10},{10,1... | collective-permute-start | bytes 9224 | tf_op jit(solution)/shard_map/ppermute | solution.py:27
  234.7 4.8 %collective-permute-start.35 = (f32[6,128]{1,0:T(8,128)S(1)}, f32[6,128]{1,0:T(8,128)S(1)}, u32[]{:S(2)}, u32[]{:S(2)}) collective-permute-start(f32[6,128]{1,0:T(8,128)S(1)} %add_add_fusion.1), channel_id=1, source_target_pairs={{0,3},{1,0},{2,1},{3,2},{4,7},{5,4},{6,5},{7,6},{8,11},{9,8},{10,9... | collective-permute-start | bytes 9224 | tf_op jit(solution)/shard_map/ppermute | solution.py:27
